TPU v7x, 32 devices: a whole 2x2x4 slice. The times are simulated.
32 devices in a mesh: gx: 2 (over y), gy: 4 (over x, core), gz: 4 (over z).
Axes of the slice: x: 2, y: 2, z: 4, core: 2. Of those that a mesh axis runs over, the one named last changes fastest.
Arguments:
- tokens: bfloat16 [256, 8192], P('gx', 'gy'), may hold values from -6 to 6
- cotangent: bfloat16 [256, 8192], P('gx', 'gy'), may hold values from -6 to 6
- gate_weight: bfloat16 [8192, 28672], P('gy', ('gx', 'gz')), may hold values from -5.7452426 to 5.7452426
- up_weight: bfloat16 [8192, 28672], P('gy', ('gx', 'gz')), may hold values from -5.7452426 to 5.7452426
- down_weight: bfloat16 [28672, 8192], P(('gx', 'gz'), 'gy'), may hold values from -3.0709613 to 3.0709613
- gate_reduce: bfloat16 [8192, 32], P('gy'), may hold values from -0.0625 to 0.0625
- gate_expand: bfloat16 [32, 28672], P(None, ('gx', 'gz')), may hold values from -5 to 5
- gate_magnitude: float32 [28672], P(('gx', 'gz')), may hold values from 0.5 to 2
- up_reduce: bfloat16 [8192, 32], P('gy'), may hold values from -0.0625 to 0.0625
- up_expand: bfloat16 [32, 28672], P(None, ('gx', 'gz')), may hold values from -5 to 5
- up_magnitude: float32 [28672], P(('gx', 'gz')), may hold values from 0.5 to 2
- down_reduce: bfloat16 [28672, 32], P(('gx', 'gz')), may hold values from -0.03125 to 0.03125
- down_expand: bfloat16 [32, 8192], P(None, 'gy'), may hold values from -5 to 5
- down_magnitude: float32 [8192], P('gy'), may hold values from 0.5 to 2
Outputs:
- output: bfloat16 [256, 8192], P('gx', 'gy')
- grad_tokens: bfloat16 [256, 8192], P('gx', 'gy')
- grad_gate_reduce: float32 [8192, 32], P('gy')
- grad_gate_expand: float32 [32, 28672], P(None, ('gx', 'gz'))
- grad_gate_magnitude: float32 [28672], P(('gx', 'gz'))
- grad_up_reduce: float32 [8192, 32], P('gy')
- grad_up_expand: float32 [32, 28672], P(None, ('gx', 'gz'))
- grad_up_magnitude: float32 [28672], P(('gx', 'gz'))
- grad_down_reduce: float32 [28672, 32], P(('gx', 'gz'))
- grad_down_expand: float32 [32, 8192], P(None, 'gy')
- grad_down_magnitude: float32 [8192], P('gy')
All inputs are finite; a program needn't handle non-finite values.
Results may differ from a plain program's by a relative error of at most 0.012.
Values may be sent and summed in bfloat16 or wider, within the bound.
A program may use at most 128 MiB of HBM per device.

v0:
```python
import jax
import jax.numpy as jnp
from jax import lax
from jax.sharding import PartitionSpec as P

EPSILON = 1e-06


def tile_square(weight, reduce_in, expand_out):
    merged = weight.astype(jnp.float32) + jnp.dot(
        reduce_in, expand_out, preferred_element_type=jnp.float32
    )
    return jnp.sum(merged * merged, axis=0)


def share_rows(values, count):
    return lax.dynamic_slice_in_dim(values, lax.axis_index("gz") * count, count, 0)


def contract_last(left, right):
    return lax.dot_general(
        left, right, (((1,), (1,)), ((), ())), preferred_element_type=jnp.float32
    )


def contract_first(left, right):
    return lax.dot_general(
        left, right, (((0,), (0,)), ((), ())), preferred_element_type=jnp.float32
    )


def scatter_pair(part, low_part, axes):
    width = part.shape[1]
    joined = jnp.concatenate(
        [part.astype(jnp.bfloat16), low_part.astype(jnp.bfloat16)], axis=1
    )
    summed = lax.psum_scatter(joined, axes, scatter_dimension=0, tiled=True)
    return summed[:, :width].astype(jnp.float32), summed[:, width:]


def on_device(
    tokens,
    cotangent,
    gate_weight,
    up_weight,
    down_weight,
    gate_reduce,
    gate_expand,
    gate_magnitude,
    up_reduce,
    up_expand,
    up_magnitude,
    down_reduce,
    down_expand,
    down_magnitude,
):
    share_count = tokens.shape[0] // lax.axis_size("gz")
    square_gate = tile_square(gate_weight, gate_reduce, gate_expand)
    square_up = tile_square(up_weight, up_reduce, up_expand)
    square_down = tile_square(down_weight, down_reduce, down_expand)
    norm_down = jnp.sqrt(lax.psum(square_down, ("gx", "gz")) + EPSILON)
    scale_down = down_magnitude / norm_down
    all_tokens = lax.all_gather(tokens, "gx", axis=0, tiled=True)
    part_gate = jnp.dot(all_tokens, gate_weight, preferred_element_type=jnp.float32)
    part_up = jnp.dot(all_tokens, up_weight, preferred_element_type=jnp.float32)
    low_gate_part = jnp.dot(all_tokens, gate_reduce, preferred_element_type=jnp.float32)
    low_up_part = jnp.dot(all_tokens, up_reduce, preferred_element_type=jnp.float32)
    gate_lin, gate_low = scatter_pair(part_gate, low_gate_part, "gy")
    up_lin, up_low = scatter_pair(part_up, low_up_part, "gy")
    summed_gate, summed_up = lax.psum((square_gate, square_up), "gy")
    norm_gate = jnp.sqrt(summed_gate + EPSILON)
    norm_up = jnp.sqrt(summed_up + EPSILON)
    scale_gate = gate_magnitude / norm_gate
    scale_up = up_magnitude / norm_up
    gate_lin = gate_lin + jnp.dot(gate_low, gate_expand, preferred_element_type=jnp.float32)
    up_lin = up_lin + jnp.dot(up_low, up_expand, preferred_element_type=jnp.float32)
    gate_pre = gate_lin * scale_gate[None, :]
    up_pre = up_lin * scale_up[None, :]
    sigmoid_gate = jax.nn.sigmoid(gate_pre)
    active = gate_pre * sigmoid_gate
    hidden = (active * up_pre).astype(jnp.bfloat16)
    all_hidden = lax.all_gather(hidden, "gy", axis=0, tiled=True)
    part_down = jnp.dot(all_hidden, down_weight, preferred_element_type=jnp.float32)
    low_down_part = jnp.dot(all_hidden, down_reduce, preferred_element_type=jnp.float32)
    down_lin, down_low = scatter_pair(part_down, low_down_part, ("gx", "gz"))
    down_lin = down_lin + jnp.dot(down_low, down_expand, preferred_element_type=jnp.float32)
    output = lax.all_gather(
        (down_lin * scale_down[None, :]).astype(jnp.bfloat16), "gz", axis=0, tiled=True
    )
    cot_float = cotangent.astype(jnp.float32)
    down_delta = (cot_float * scale_down[None, :]).astype(jnp.bfloat16)
    cot_share = share_rows(cot_float, share_count)
    delta_share = share_rows(down_delta, share_count)
    grad_down_magnitude = jnp.sum(cot_share * down_lin, axis=0) / norm_down
    grad_down_expand = contract_first(down_low, delta_share)
    grad_down_magnitude, grad_down_expand = lax.psum(
        (grad_down_magnitude, grad_down_expand), ("gx", "gz")
    )
    all_delta = lax.all_gather(down_delta, "gx", axis=0, tiled=True)
    part_hidden_grad = contract_last(all_delta, down_weight)
    part_down_back = contract_last(all_delta, down_expand)
    hidden_gradsum, down_back = scatter_pair(part_hidden_grad, part_down_back, "gy")
    hidden_grad = (hidden_gradsum + contract_last(down_back, down_reduce)).astype(jnp.bfloat16)
    hgrad_float = hidden_grad.astype(jnp.float32)
    gate_grad = hgrad_float * up_pre * sigmoid_gate * (1.0 + gate_pre * (1.0 - sigmoid_gate))
    up_grad = hgrad_float * active
    gate_delta = (gate_grad * scale_gate[None, :]).astype(jnp.bfloat16)
    up_delta = (up_grad * scale_up[None, :]).astype(jnp.bfloat16)
    grad_gate_magnitude = jnp.sum(gate_grad * gate_lin, axis=0) / norm_gate
    grad_up_magnitude = jnp.sum(up_grad * up_lin, axis=0) / norm_up
    grad_gate_magnitude, grad_up_magnitude = lax.psum(
        (grad_gate_magnitude, grad_up_magnitude), "gy"
    )
    rank = gate_low.shape[1]
    all_low = lax.all_gather(
        jnp.concatenate([gate_low, up_low, down_back], axis=1), "gy", axis=0, tiled=True
    )
    all_gate_delta, all_up_delta = (
        lax.all_gather(gate_delta, "gy", axis=0, tiled=True),
        lax.all_gather(up_delta, "gy", axis=0, tiled=True),
    )
    grad_gate_expand = contract_first(all_low[:, :rank], all_gate_delta)
    grad_up_expand = contract_first(all_low[:, rank : 2 * rank], all_up_delta)
    grad_down_reduce = contract_first(all_hidden, all_low[:, 2 * rank :])
    part_input = contract_last(all_gate_delta, gate_weight) + contract_last(all_up_delta, up_weight)
    part_gate_back = contract_last(all_gate_delta, gate_expand)
    part_up_back = contract_last(all_up_delta, up_expand)
    input_sum, back_pair = scatter_pair(
        part_input, jnp.concatenate([part_gate_back, part_up_back], axis=1), ("gx", "gz")
    )
    gate_back = back_pair[:, :rank]
    up_back = back_pair[:, rank:]
    grad_tokens = lax.all_gather(
        (
            input_sum + contract_last(gate_back, gate_reduce) + contract_last(up_back, up_reduce)
        ).astype(jnp.bfloat16),
        "gz",
        axis=0,
        tiled=True,
    )
    token_share = share_rows(tokens, share_count)
    grad_gate_reduce = contract_first(token_share, gate_back)
    grad_up_reduce = contract_first(token_share, up_back)
    grad_gate_reduce, grad_up_reduce = lax.psum((grad_gate_reduce, grad_up_reduce), ("gx", "gz"))
    return (
        output,
        grad_tokens,
        grad_gate_reduce,
        grad_gate_expand,
        grad_gate_magnitude,
        grad_up_reduce,
        grad_up_expand,
        grad_up_magnitude,
        grad_down_reduce,
        grad_down_expand,
        grad_down_magnitude,
    )


def solution(mesh):
    return jax.shard_map(
        on_device,
        mesh=mesh,
        in_specs=(
            P("gx", "gy"),
            P("gx", "gy"),
            P("gy", ("gx", "gz")),
            P("gy", ("gx", "gz")),
            P(("gx", "gz"), "gy"),
            P("gy", None),
            P(None, ("gx", "gz")),
            P(("gx", "gz")),
            P("gy", None),
            P(None, ("gx", "gz")),
            P(("gx", "gz")),
            P(("gx", "gz"), None),
            P(None, "gy"),
            P("gy"),
        ),
        out_specs=(
            P("gx", "gy"),
            P("gx", "gy"),
            P("gy", None),
            P(None, ("gx", "gz")),
            P(("gx", "gz")),
            P("gy", None),
            P(None, ("gx", "gz")),
            P(("gx", "gz")),
            P(("gx", "gz"), None),
            P(None, "gy"),
            P("gy"),
        ),
        check_vma=False,
    )
```

profile of v0, /device:TPU:0, one launch (start us, length us, event | category | flops | bytes accessed | tf_op | source)
XLA Modules:
  0.0 484.8 jit_solution(14400527635219702178)
XLA Ops:
  7.3 9.5 %multiply_reduce_fusion = f32[2048]{0:T(1024)S(1)} fusion(bf16[3584,2048]{1,0:T(8,128)(2,1)} %param.18, bf16[3584,32]{0,1:T(8,128)(2,1)} %param.25, bf16[32,2048]{1,0:T(8,128)(2,1)} %param.26), kind=kOutput, calls=%fused_computation | convolution fusion | flops 499120128 | bytes 15048704 | tf_op jit(solution)/shard_map/dot_general | solution.py:10
  16.7 23.7 %psum.65 = f32[2048]{0:T(1024)S(1)} all-reduce(f32[2048]{0:T(1024)S(1)} %multiply_reduce_fusion), channel_id=1, replica_groups=mesh['gx'=2,'gy'=4,'gz'=4] {'gx','gz'}, use_global_device_ids=true, to_apply=%region_8.0 | all-reduce | flops 2048 | bytes 16384 | tf_op jit(solution)/shard_map/psum | solution.py:61
  42.3 17.9 %all-gather.10.cloned.1.call-done = bf16[256,2048]{1,0:T(8,128)(2,1)} async-done(((bf16[128,2048]{1,0:T(8,128)(2,1)}), bf16[256,2048]{1,0:T(8,128)(2,1)}) %all-gather.10.cloned.1.call-update) | async-done | bytes 1048592 | tf_op jit(solution)/shard_map/all_gather | solution.py:99
  60.2 9.6 %convolution_convert_fusion = bf16[256,3584]{1,0:T(8,128)(2,1)S(1)} fusion(bf16[256,2048]{1,0:T(8,128)(2,1)} %all-gather.10.cloned.1.call-done, bf16[3584,2048]{1,0:T(8,128)(2,1)} %param.18), kind=kOutput, calls=%fused_computation.3 | convolution fusion | flops 3759013888 | bytes 17563648 | tf_op jit(solution)/shard_map/dot_general | solution.py:21
  71.8 11.2 %all-gather.6.cloned.1.call-done = bf16[256,2048]{1,0:T(8,128)(2,1)} async-done(((bf16[128,2048]{1,0:T(8,128)(2,1)}), bf16[256,2048]{1,0:T(8,128)(2,1)}) %all-gather.6.cloned.1.call-update) | async-done | bytes 1048592 | tf_op jit(solution)/shard_map/all_gather | solution.py:63
  84.8 9.5 %convolution_convert_fusion.2 = bf16[256,3584]{1,0:T(8,128)(2,1)S(1)} fusion(bf16[256,2048]{1,0:T(8,128)(2,1)} %all-gather.6.cloned.1.call-done, bf16[2048,3584]{1,0:T(8,128)(2,1)} %param.16), kind=kOutput, calls=%fused_computation.5 | convolution fusion | flops 3759013888 | bytes 17563648 | tf_op jit(solution)/shard_map/dot_general | solution.py:64
  96.6 9.1 %convolution_convert_fusion.1 = bf16[256,3584]{1,0:T(8,128)(2,1)S(1)} fusion(bf16[256,2048]{1,0:T(8,128)(2,1)S(1)} %copy-done.4, bf16[2048,3584]{1,0:T(8,128)(2,1)} %param.17), kind=kOutput, calls=%fused_computation.4 | convolution fusion | flops 3759013888 | bytes 17563648 | tf_op jit(solution)/shard_map/dot_general | solution.py:65
  107.2 7.6 %multiply_reduce_fusion.2 = f32[3584]{0:T(1024)S(1)} fusion(bf16[2048,3584]{1,0:T(8,128)(2,1)} %param.16, bf16[2048,32]{0,1:T(8,128)(2,1)S(1)} %copy-done.13, bf16[32,3584]{1,0:T(8,128)(2,1)S(1)} %copy-done.9), kind=kOutput, calls=%fused_computation.2 | convolution fusion | flops 499118592 | bytes 15054848 | tf_op jit(solution)/shard_map/dot_general | solution.py:10
  114.8 7.6 %multiply_reduce_fusion.1 = f32[3584]{0:T(1024)S(1)} fusion(bf16[2048,3584]{1,0:T(8,128)(2,1)} %param.17, bf16[2048,32]{0,1:T(8,128)(2,1)S(1)} %copy-done.15, bf16[32,3584]{1,0:T(8,128)(2,1)S(1)} %copy-done), kind=kOutput, calls=%fused_computation.1 | convolution fusion | flops 499118592 | bytes 15054848 | tf_op jit(solution)/shard_map/dot_general | solution.py:10
  122.4 10.9 %all-reduce.2 = (f32[3584]{0:T(1024)S(1)}, f32[3584]{0:T(1024)S(1)}) all-reduce(f32[3584]{0:T(1024)S(1)} %multiply_reduce_fusion.1, f32[3584]{0:T(1024)S(1)} %multiply_reduce_fusion.2), channel_id=1, replica_groups=mesh['gx'=2,'gy'=4,'gz'=4] {'gy'}, use_global_device_ids=true, to_apply=%region_5.0 | all-reduce | flops 7168 | bytes 57344 | tf_op jit(solution)/shard_map/psum | solution.py:70
  135.4 12.6 %reduce-scatter.6.cloned.1.call-done = bf16[64,3616]{1,0:T(8,128)(2,1)} async-done(((bf16[256,3616]{1,0:T(8,128)(2,1)}), bf16[64,3616]{1,0:T(8,128)(2,1)}) %reduce-scatter.6.cloned.1.call-update) | async-done | bytes 462864 | tf_op jit(solution)/shard_map/reduce_scatter | solution.py:37
  149.3 31.1 %reduce-scatter.8.cloned.1.call-done = bf16[64,3616]{1,0:T(8,128)(2,1)} async-done(((bf16[256,3616]{1,0:T(8,128)(2,1)}), bf16[64,3616]{1,0:T(8,128)(2,1)}) %reduce-scatter.8.cloned.1.call-update) | async-done | bytes 462864 | tf_op jit(solution)/shard_map/reduce_scatter | solution.py:37
  180.5 3.4 multiply_reduce_fusion.3
  185.6 19.5 %all-gather.14.cloned.1.call-done = bf16[256,3584]{1,0:T(8,128)(2,1)} async-done(((bf16[64,3584]{1,0:T(8,128)(2,1)}), bf16[256,3584]{1,0:T(8,128)(2,1)}) %all-gather.14.cloned.1.call-update) | async-done | bytes 1835024 | tf_op jit(solution)/shard_map/all_gather | solution.py:120
  205.1 2.1 convolution_convert_fusion.4
  207.4 21.0 %all-gather.8.cloned.1.call-done = bf16[256,3584]{1,0:T(8,128)(2,1)} async-done(((bf16[64,3584]{1,0:T(8,128)(2,1)}), bf16[256,3584]{1,0:T(8,128)(2,1)}) %all-gather.8.cloned.1.call-update) | async-done | bytes 1835024 | tf_op jit(solution)/shard_map/all_gather | solution.py:82
  228.4 2.2 convolution_convert_fusion.7
  230.8 20.9 %all-gather.12.cloned.1.call-done = bf16[256,3584]{1,0:T(8,128)(2,1)} async-done(((bf16[64,3584]{1,0:T(8,128)(2,1)}), bf16[256,3584]{1,0:T(8,128)(2,1)}) %all-gather.12.cloned.1.call-update) | async-done | bytes 1835024 | tf_op jit(solution)/shard_map/all_gather | solution.py:119
  251.7 2.1 convolution_convert_fusion.5
  253.9 7.5 %convolution_convert_fusion.3 = bf16[256,2048]{1,0:T(8,128)(2,1)S(1)} fusion(bf16[256,3584]{1,0:T(8,128)(2,1)S(1)} %copy-done.2, bf16[3584,2048]{1,0:T(8,128)(2,1)} %param.18), kind=kOutput, calls=%fused_computation.13 | convolution fusion | flops 3758620672 | bytes 17563648 | tf_op jit(solution)/shard_map/dot_general | solution.py:83
  263.0 11.2 %fusion.35 = f32[256,2048]{1,0:T(8,128)} fusion(bf16[256,3584]{1,0:T(8,128)(2,1)} %all-gather.12.cloned.1.call-done, bf16[2048,3584]{1,0:T(8,128)(2,1)} %param.16), kind=kOutput, calls=%fused_computation.73 | convolution fusion | flops 3758096384 | bytes 18612224 | tf_op jit(solution)/shard_map/dot_general | solution.py:21
  274.2 15.9 %fusion.2 = bf16[256,2048]{1,0:T(8,128)(2,1)} fusion(f32[256,2048]{1,0:T(8,128)} %fusion.35, bf16[256,3584]{1,0:T(8,128)(2,1)S(1)} %copy-done.1, bf16[2048,3584]{1,0:T(8,128)(2,1)} %param.17), kind=kOutput, calls=%fused_computation.12 | convolution fusion | flops 3759144960 | bytes 19660800 | tf_op jit(solution)/shard_map/dot_general | solution.py:21
  290.1 3.1 concatenate.25
  294.4 11.3 %all-reduce.1 = (f32[3584]{0:T(1024)}, f32[3584]{0:T(1024)}) all-reduce(f32[3584]{0:T(1024)S(1)} %get-tuple-element.25, f32[3584]{0:T(1024)S(1)} %get-tuple-element.26), channel_id=1, replica_groups=mesh['gx'=2,'gy'=4,'gz'=4] {'gy'}, use_global_device_ids=true, to_apply=%region_13.0 | all-reduce | flops 7168 | bytes 57344 | tf_op jit(solution)/shard_map/psum | solution.py:111
  305.8 5.2 %all_gather.31 = bf16[256,96]{1,0:T(8,128)(2,1)S(1)} all-gather(bf16[64,96]{1,0:T(8,128)(2,1)S(1)} %pad_maximum_fusion.4), channel_id=1, replica_groups=mesh['gx'=2,'gy'=4,'gz'=4] {'gy'}, dimensions={0}, use_global_device_ids=true | all-gather | bytes 61440 | tf_op jit(solution)/shard_map/all_gather | solution.py:115
  311.1 2.8 fusion.15
  316.5 11.0 %reduce-scatter.10.cloned.1.call-done = bf16[32,2080]{1,0:T(8,128)(2,1)} async-done(((bf16[256,2080]{1,0:T(8,128)(2,1)}), bf16[32,2080]{1,0:T(8,128)(2,1)}) %reduce-scatter.10.cloned.1.call-update) | async-done | bytes 133136 | tf_op jit(solution)/shard_map/reduce_scatter | solution.py:37
  328.7 17.7 %all_gather.26 = bf16[128,2048]{1,0:T(8,128)(2,1)S(1)} all-gather(bf16[32,2048]{1,0:T(8,128)(2,1)S(1)} %get-tuple-element.24), channel_id=1, replica_groups=mesh['gx'=2,'gy'=4,'gz'=4] {'gz'}, dimensions={0}, use_global_device_ids=true | all-gather | bytes 655360 | tf_op jit(solution)/shard_map/all_gather | solution.py:87
  348.2 46.4 %reduce-scatter.14.cloned.1.call-done = bf16[32,2112]{1,0:T(8,128)(2,1)} async-done(((bf16[256,2112]{1,0:T(8,128)(2,1)}), bf16[32,2112]{1,0:T(8,128)(2,1)}) %reduce-scatter.14.cloned.1.call-update) | async-done | bytes 135184 | tf_op jit(solution)/shard_map/reduce_scatter | solution.py:37
  398.0 20.4 %psum.71 = f32[2048]{0:T(1024)} all-reduce(f32[2048]{0:T(1024)S(1)} %fusion.21), channel_id=1, replica_groups=mesh['gx'=2,'gy'=4,'gz'=4] {'gx','gz'}, use_global_device_ids=true, to_apply=%region_19.0 | all-reduce | flops 2048 | bytes 16384 | tf_op jit(solution)/shard_map/psum | solution.py:96
  420.5 16.5 %all_gather.30 = bf16[128,2048]{1,0:T(8,128)(2,1)S(1)} all-gather(bf16[32,2048]{1,0:T(8,128)(2,1)S(1)} %fusion.3), channel_id=1, replica_groups=mesh['gx'=2,'gy'=4,'gz'=4] {'gz'}, dimensions={0}, use_global_device_ids=true | all-gather | bytes 655360 | tf_op jit(solution)/shard_map/all_gather | solution.py:133
  437.0 37.6 %all-reduce.5.cloned.1.call-done = (f32[2048,32]{0,1:T(8,128)}, f32[2048,32]{0,1:T(8,128)}, f32[32,2048]{1,0:T(8,128)}) async-done(((f32[2048,32]{0,1:T(8,128)}, f32[2048,32]{0,1:T(8,128)}, f32[32,2048]{1,0:T(8,128)}), (f32[2048,32]{0,1:T(8,128)}, f32[2048,32]{0,1:T(8,128)}, f32[32,2048]{1,0:T(8,128)})) %all-reduce.5.cloned.1.call-update) | async-done | bytes 786448 | tf_op jit(solution)/shard_map/psum | solution.py:144
  (120 shorter events, 32.3 us)
Async XLA Ops:
  7.2 107.6 %copy-start = (bf16[32,3584]{1,0:T(8,128)(2,1)S(1)}, bf16[32,3584]{1,0:T(8,128)(2,1)}, u32[]{:S(2)}) copy-start(bf16[32,3584]{1,0:T(8,128)(2,1)} %param.23) | copy-start | bytes 688132
  7.2 33.3 %copy-start.26 = (f32[2048]{0:T(1024)S(1)}, f32[2048]{0:T(1024)}, u32[]{:S(2)}) copy-start(f32[2048]{0:T(1024)} %param.27) | copy-start | bytes 24580
  7.2 33.3 %copy-start.5 = (bf16[128,2048]{1,0:T(8,128)(2,1)S(1)}, bf16[128,2048]{1,0:T(8,128)(2,1)}, u32[]{:S(2)}) copy-start(bf16[128,2048]{1,0:T(8,128)(2,1)} %param.15) | copy-start | bytes 1572868
  7.2 52.9 %all-gather.10.cloned.1.call-start = ((), (), s32[]{:S(2)}) async-start(), calls=%async_computation.10 | async-start | bytes 1572864 | tf_op jit(solution)/shard_map/all_gather | solution.py:99
  41.5 41.5 %all-gather.6.cloned.1.call-start = ((), (), s32[]{:S(2)}) async-start(), calls=%async_computation.5 | async-start | bytes 1572864 | tf_op jit(solution)/shard_map/all_gather | solution.py:63
  42.2 27.5 %copy-start.11 = (bf16[32,2048]{1,0:T(8,128)(2,1)S(1)}, bf16[32,2048]{1,0:T(8,128)(2,1)}, u32[]{:S(2)}) copy-start(bf16[32,2048]{1,0:T(8,128)(2,1)} %param.26) | copy-start | bytes 393220
  42.2 91.8 %reduce-scatter.12.cloned.1.call-start = ((), (), s32[]{:S(2)}) async-start(), calls=%async_computation.11 | async-start | bytes 2375680 | tf_op jit(solution)/shard_map/reduce_scatter | solution.py:37
  60.2 9.6 %copy-start.7 = (bf16[256,2048]{1,0:T(8,128)(2,1)S(1)}, bf16[256,2048]{1,0:T(8,128)(2,1)}, u32[]{:S(2)}) copy-start(bf16[256,2048]{1,0:T(8,128)(2,1)} %all-gather.10.cloned.1.call-done) | copy-start | bytes 3145732
  70.3 12.7 %copy-start.13 = (bf16[2048,32]{0,1:T(8,128)(2,1)S(1)}, bf16[2048,32]{0,1:T(8,128)(2,1)}, u32[]{:S(2)}) copy-start(bf16[2048,32]{0,1:T(8,128)(2,1)} %param.19) | copy-start | bytes 393220
  71.7 76.3 %reduce-scatter.6.cloned.1.call-start = ((), (), s32[]{:S(2)}) async-start(), calls=%async_computation.6 | async-start | bytes 2375680 | tf_op jit(solution)/shard_map/reduce_scatter | solution.py:37
  95.7 84.8 %reduce-scatter.8.cloned.1.call-start = ((), (), s32[]{:S(2)}) async-start(), calls=%async_computation.7 | async-start | bytes 2375680 | tf_op jit(solution)/shard_map/reduce_scatter | solution.py:37
  107.2 98.0 %all-gather.14.cloned.1.call-start = ((), (), s32[]{:S(2)}) async-start(), calls=%async_computation.13 | async-start | bytes 2293760 | tf_op jit(solution)/shard_map/all_gather | solution.py:120
  114.8 18.6 %copy-start.22 = (f32[3584]{0:T(1024)S(1)}, f32[3584]{0:T(1024)}, u32[]{:S(2)}) copy-start(f32[3584]{0:T(1024)} %param.21) | copy-start | bytes 43012
  114.8 18.6 %copy-start.23 = (f32[3584]{0:T(1024)S(1)}, f32[3584]{0:T(1024)}, u32[]{:S(2)}) copy-start(f32[3584]{0:T(1024)} %param.24) | copy-start | bytes 43012
  114.8 19.2 %copy-start.8 = (bf16[3584,32]{0,1:T(8,128)(2,1)S(1)}, bf16[3584,32]{0,1:T(8,128)(2,1)}, u32[]{:S(2)}) copy-start(bf16[3584,32]{0,1:T(8,128)(2,1)} %param.25) | copy-start | bytes 688132
  183.9 44.5 %all-gather.8.cloned.1.call-start = ((), (), s32[]{:S(2)}) async-start(), calls=%async_computation.8 | async-start | bytes 2293760 | tf_op jit(solution)/shard_map/all_gather | solution.py:82
  184.6 67.0 %all-gather.12.cloned.1.call-start = ((), (), s32[]{:S(2)}) async-start(), calls=%async_computation.12 | async-start | bytes 2293760 | tf_op jit(solution)/shard_map/all_gather | solution.py:119
  185.5 66.1 %copy-start.10 = (bf16[32,3584]{1,0:T(8,128)(2,1)S(1)}, bf16[32,3584]{1,0:T(8,128)(2,1)}, u32[]{:S(2)}) copy-start(bf16[32,3584]{1,0:T(8,128)(2,1)} %param.20) | copy-start | bytes 688132
  185.6 141.9 %reduce-scatter.10.cloned.1.call-start = ((), (), s32[]{:S(2)}) async-start(), calls=%async_computation.9 | async-start | bytes 1253376 | tf_op jit(solution)/shard_map/reduce_scatter | solution.py:37
  228.4 25.5 %copy-start.2 = (bf16[256,3584]{1,0:T(8,128)(2,1)S(1)}, bf16[256,3584]{1,0:T(8,128)(2,1)}, u32[]{:S(2)}) copy-start(bf16[256,3584]{1,0:T(8,128)(2,1)} %all-gather.8.cloned.1.call-done) | copy-start | bytes 5505028
  262.7 11.5 %copy-start.1 = (bf16[256,3584]{1,0:T(8,128)(2,1)S(1)}, bf16[256,3584]{1,0:T(8,128)(2,1)}, u32[]{:S(2)}) copy-start(bf16[256,3584]{1,0:T(8,128)(2,1)} %all-gather.14.cloned.1.call-done) | copy-start | bytes 5505028
  262.7 131.9 %reduce-scatter.14.cloned.1.call-start = ((), (), s32[]{:S(2)}) async-start(), calls=%async_computation.14 | async-start | bytes 1253376 | tf_op jit(solution)/shard_map/reduce_scatter | solution.py:37
  290.1 4.3 copy-start.24
  290.1 4.3 copy-start.25
  290.1 15.6 %slice-start = ((bf16[64,3616]{1,0:T(8,128)(2,1)}), bf16[64,32]{1,0:T(8,128)(2,1)S(1)}, s32[]{:S(2)}) async-start(bf16[64,3616]{1,0:T(8,128)(2,1)} %reduce-scatter.12.cloned.1.call-done), calls=%async_computation.16 | async-start | bytes 32768 | tf_op jit(solution)/shard_map/slice | solution.py:38
  290.1 15.6 %slice-start.1 = ((bf16[64,3616]{1,0:T(8,128)(2,1)}), bf16[64,32]{1,0:T(8,128)(2,1)S(1)}, s32[]{:S(2)}) async-start(bf16[64,3616]{1,0:T(8,128)(2,1)} %reduce-scatter.8.cloned.1.call-done), calls=%async_computation.17 | async-start | bytes 32768 | tf_op jit(solution)/shard_map/slice | solution.py:38
  290.1 15.6 %slice-start.2 = ((bf16[64,3616]{1,0:T(8,128)(2,1)}), bf16[64,32]{1,0:T(8,128)(2,1)S(1)}, s32[]{:S(2)}) async-start(bf16[64,3616]{1,0:T(8,128)(2,1)} %reduce-scatter.6.cloned.1.call-done), calls=%async_computation.18 | async-start | bytes 32768 | tf_op jit(solution)/shard_map/slice | solution.py:38
  293.2 181.3 %all-reduce.5.cloned.1.call-start = ((), (), s32[]{:S(2)}) async-start(), calls=%async_computation.15 | async-start | bytes 1572864 | tf_op jit(solution)/shard_map/psum | solution.py:144
  313.9 13.5 %copy-start.12 = (bf16[32,2048]{1,0:T(8,128)(2,1)S(1)}, bf16[32,2048]{1,0:T(8,128)(2,1)}, u32[]{:S(2)}) copy-start(bf16[32,2048]{1,0:T(8,128)(2,1)} %param.26) | copy-start | bytes 393220
  315.2 79.4 %copy-start.6 = (bf16[128,2048]{1,0:T(8,128)(2,1)S(1)}, bf16[128,2048]{1,0:T(8,128)(2,1)}, u32[]{:S(2)}) copy-start(bf16[128,2048]{1,0:T(8,128)(2,1)} %param.14) | copy-start | bytes 1572868
  316.5 101.9 %copy-start.14 = (bf16[2048,32]{0,1:T(8,128)(2,1)S(1)}, bf16[2048,32]{0,1:T(8,128)(2,1)}, u32[]{:S(2)}) copy-start(bf16[2048,32]{0,1:T(8,128)(2,1)} %param.19) | copy-start | bytes 393220
  316.5 103.0 %copy-start.16 = (bf16[2048,32]{0,1:T(8,128)(2,1)S(1)}, bf16[2048,32]{0,1:T(8,128)(2,1)}, u32[]{:S(2)}) copy-start(bf16[2048,32]{0,1:T(8,128)(2,1)} %param.22) | copy-start | bytes 393220
  (9 other events, 22.4 us)
Sparse Core Ops, SparseCore 0:
  41.6 18.5 all-gather.9
  61.7 21.2 all-gather.5
  85.6 29.9 reduce-scatter.11
  118.0 30.0 reduce-scatter.5
  150.4 29.9 reduce-scatter.7
  184.0 21.0 all-gather.13
  207.3 21.0 all-gather.7
  230.5 21.0 all-gather.11
  262.8 64.5 reduce-scatter.9
  330.7 63.8 reduce-scatter.13
  399.5 75.0 all-reduce.4
where the time goes:
time: 486 us; the launch traced here: 485 us
  waiting for transfers between devices  231 us (48%)
  matrix products  116 us (24%)
  blocking collectives  106 us (22%)
  between operations  14.3 us (3%)
  other arithmetic  8.95 us (2%)
  local copies, waits for them, and re-layouts  7.88 us (2%)
    reduce_scatter x5, waiting for transfers between devices, scatter_pair(): summed = lax.psum_scatter(joined, axes, scatter_dimension=0, tiled=True)  101 us
    dot_general x9, matrix products, contract_last(): lax.dot_general(left, right, (((1,), (1,)), ((), ())), preferred_element_...  44.7 us
    psum x1, waiting for transfers between devices, on_device(): lax.psum((grad_gate_reduce, grad_up_reduce), ('gx', 'gz'))  37.6 us
    dot_general x3, matrix products, tile_square(): jnp.dot(reduce_in, expand_out, preferred_element_type=jnp.float32)  24.6 us
    psum x1, blocking collectives, on_device(): norm_down = jnp.sqrt(lax.psum(square_down, ('gx', 'gz')) + EPSILON)  23.7 us
    all_gather x1, waiting for transfers between devices, on_device(): all_hidden = lax.all_gather(hidden, 'gy', axis=0, tiled=True)  21 us
    all_gather x1, waiting for transfers between devices, on_device(): lax.all_gather(gate_delta, 'gy', axis=0, tiled=True)  20.9 us
    psum x1, blocking collectives, on_device(): lax.psum((grad_down_magnitude, grad_down_expand), ('gx', 'gz'))  20.4 us
  transfers between devices with their start and end apart: 11, of which 10 were waited for; matrix products, arithmetic and copies ran while one was open for 21% of the time, Pallas kernels for 0%

commit v1 on v0

--- a/solution.py
+++ b/solution.py
@@ -1,9 +1,15 @@
+import functools
+
 import jax
 import jax.numpy as jnp
 from jax import lax
+from jax.experimental import pallas as pl
+from jax.experimental.pallas import tpu as pltpu
 from jax.sharding import PartitionSpec as P
 
 EPSILON = 1e-06
+BF16 = jnp.bfloat16
+F32 = jnp.float32
 
 
 def tile_square(weight, reduce_in, expand_out):
@@ -157,9 +163,793 @@
     )
 
 
+LANES = 128
+
+
+def dot(left, right):
+    return jnp.dot(left, right, preferred_element_type=F32)
+
+
+def kernel(
+    tok_hbm, cot_hbm, wg_hbm, wu_hbm, wd_hbm, ag_hbm, au_hbm, bd_hbm, bg_hbm, bu_hbm, ad_hbm,
+    mg_hbm, mu_hbm, md_hbm,
+    out_hbm, gtok_hbm, grg_hbm, gru_hbm, gde_hbm, geg_hbm, geu_hbm, gdr_hbm,
+    gmg_hbm, gmu_hbm, gdm_hbm,
+    wide, deep, m_gu, m_d, gm_out, gd_out,
+    wg, wu, wd, xt, dl, part, xr, hid, cs, acc, ysend, ykeep, yrecv, z1r, z2r,
+    obuf, cot_mine, low, la, lar, back, lb, lbr, nds, ngs, scale_gu, gms, gmr, gds, extra,
+    w_sem, in_sem, in_send, in_recv, cs_sem, c_recv, x_send, x_recv, ag_send, ag_recv,
+    yz_send, yz_recv, nd_send, gd_send, nd_recv, ng_send, ng_recv, la_send, la_recv,
+    lb_send, lb_recv, gm_sem, out_sem, credit,
+):
+    gx, gy, gz = lax.axis_index("gx"), lax.axis_index("gy"), lax.axis_index("gz")
+    core = lax.rem(gy, 2)
+    bit0, bit1 = lax.rem(gz, 2), gz // 2
+    core_peer = {"gy": gy + 1 - 2 * core}
+    x_peer = {"gy": lax.rem(gy + 2, 4)}
+    y_peer = {"gx": 1 - gx}
+    z1_peer = {"gz": gz + 1 - 2 * bit0}
+    z2_peer = {"gz": lax.rem(gz + 2, 4)}
+    half_t, width = xt.shape[1], xt.shape[2]
+    quarter = half_t // 2
+    hidden_l = wg.shape[1]
+    rank = gde_hbm.shape[0]
+    fc = cs.shape[2]
+    nc = hidden_l // fc
+    dt = 512 if width % 512 == 0 else width
+    nt = width // dt
+    mine = pl.ds(pl.multiple_of(core * quarter, quarter), quarter)
+
+    def cols(c):
+        return pl.ds(pl.multiple_of(c * fc, fc), fc)
+
+    def tile(t):
+        return pl.ds(pl.multiple_of(t * dt, dt), dt)
+
+    def remote(src, dst, send, recv, peer):
+        return pltpu.make_async_remote_copy(
+            src_ref=src, dst_ref=dst, send_sem=send, recv_sem=recv,
+            device_id=peer, device_id_type=pl.DeviceIdType.MESH,
+        )
+
+    def group_peer(i):
+        place = lax.rem(gx * 4 + gz + i, 8)
+        return {"gx": place // 4, "gz": lax.rem(place, 4)}, place
+
+    barrier = pltpu.get_barrier_semaphore()
+    for i in range(1, 4):
+        pl.semaphore_signal(barrier, inc=1, device_id={"gy": lax.rem(gy + i, 4)}, device_id_type=pl.DeviceIdType.MESH)
+    for i in range(1, 8):
+        pl.semaphore_signal(barrier, inc=1, device_id=group_peer(i)[0], device_id_type=pl.DeviceIdType.MESH)
+
+    own_tok = pltpu.make_async_copy(tok_hbm, xt.at[gx], in_sem.at[0])
+    own_cot = pltpu.make_async_copy(cot_hbm, dl.at[gx], in_sem.at[1])
+    block = (bit0 * 2 + bit1) * (half_t // 4)
+    my_rows = pl.ds(pl.multiple_of(block, half_t // 4), half_t // 4)
+    cot_rows = pltpu.make_async_copy(cot_hbm.at[my_rows], cot_mine, in_sem.at[2])
+    own_tok.start()
+    factors = [
+        pltpu.make_async_copy(src, buf.at[n * rank : (n + 1) * rank], in_sem.at[3 + i])
+        for i, (src, buf, n) in enumerate((
+            (ag_hbm, wide, 0), (au_hbm, wide, 1), (bg_hbm, deep, 0), (bu_hbm, deep, 1),
+            (bd_hbm, wide, 2), (ad_hbm, deep, 2),
+        ))
+    ]
+    factors += [
+        pltpu.make_async_copy(src, dst, in_sem.at[9 + i])
+        for i, (src, dst) in enumerate(((mg_hbm, m_gu.at[0]), (mu_hbm, m_gu.at[1]), (md_hbm, m_d)))
+    ]
+    for copy in factors[:4]:
+        copy.start()
+
+    def load_w(k, c):
+        if k == 0:
+            return pltpu.make_async_copy(wg_hbm.at[:, cols(c)], wg.at[:, cols(c)], w_sem.at[0, c])
+        if k == 1:
+            return pltpu.make_async_copy(wu_hbm.at[:, cols(c)], wu.at[:, cols(c)], w_sem.at[1, c])
+        return pltpu.make_async_copy(wd_hbm.at[cols(c)], wd.at[cols(c)], w_sem.at[2, c])
+
+    for c in range(2):
+        load_w(0, c).start()
+        load_w(1, c).start()
+    for copy in factors[4:]:
+        copy.start()
+    wide[3 * rank :] = jnp.zeros((wide.shape[0] - 3 * rank, width), BF16)
+    deep[3 * rank :] = jnp.zeros((deep.shape[0] - 3 * rank, hidden_l), BF16)
+    pl.semaphore_wait(barrier, 10)
+    send_tok = remote(tok_hbm, xt.at[gx], in_send.at[0], in_recv.at[0], y_peer)
+    send_cot = remote(cot_hbm, dl.at[gx], in_send.at[1], in_recv.at[1], y_peer)
+    send_tok.start()
+    send_cot.start()
+    own_cot.start()
+    cot_rows.start()
+
+    lane = lax.broadcasted_iota(jnp.int32, (half_t, low.shape[2]), 1)
+    is_gate = lane < rank
+
+    def low_of(h):
+        low[h] = jnp.where(lane < 2 * rank, contract_last(xt[h], wide[...]), 0.0)
+
+    def unit_id(k, h, c):
+        return (k * 2 + h) * nc + c
+
+    def core_copy(k, h, c, slot):
+        return remote(
+            cs.at[slot], part.at[k, h, mine, cols(c)], cs_sem.at[slot],
+            c_recv.at[unit_id(k, h, c)], core_peer,
+        )
+
+    other_rows = pl.ds(pl.multiple_of((1 - core) * quarter, quarter), quarter)
+
+    def x_copy(k, h, c):
+        return remote(
+            part.at[k, h, mine, cols(c)], xr.at[k, h, :, cols(c)],
+            x_send.at[unit_id(k, h, c)], x_recv.at[unit_id(k, h, c)], x_peer,
+        )
+
+    def emit_unit(k, h, c, slot, value, reuse):
+        lo, hi = value[:quarter], value[quarter:]
+        part[k, h, mine, cols(c)] = jnp.where(core == 0, lo, hi).astype(BF16)
+
+        @pl.when(reuse)
+        def _():
+            core_copy(k, h, c, slot).wait_send()
+
+        cs[slot] = jnp.where(core == 0, hi, lo).astype(BF16)
+        core_copy(k, h, c, slot).start()
+
+    def finish_unit(k, h, c):
+        pltpu.make_async_remote_copy(
+            src_ref=cs.at[0], dst_ref=part.at[k, h, other_rows, cols(c)], send_sem=cs_sem.at[0],
+            recv_sem=c_recv.at[unit_id(k, h, c)], device_id=core_peer,
+            device_id_type=pl.DeviceIdType.MESH,
+        ).wait_recv()
+        total = part[k, h, mine, cols(c)].astype(F32) + part[k, h, other_rows, cols(c)].astype(F32)
+        part[k, h, mine, cols(c)] = total.astype(BF16)
+        x_copy(k, h, c).start()
+
+    def gate_up(h, first):
+        x_low = low[h]
+        low_gate = jnp.where(is_gate, x_low, 0.0).astype(BF16)
+        low_up = jnp.where(is_gate, 0.0, x_low).astype(BF16)
+
+        def body(c, _):
+            if first:
+                load_w(0, c).wait()
+                load_w(1, c).wait()
+
+                @pl.when(c + 2 < nc)
+                def _():
+                    load_w(0, c + 2).start()
+                    load_w(1, c + 2).start()
+
+                @pl.when(c + 2 >= nc)
+                def _():
+                    load_w(2, c + 2 - nc).start()
+
+            for k, w, lw in ((0, wg, low_gate), (1, wu, low_up)):
+                value = dot(xt[h], w[:, cols(c)]) + dot(lw, deep[:, cols(c)])
+                slot = lax.rem(c, 2) * 2 + k
+                emit_unit(k, h, c, slot, value, (c >= 2) if first else (c >= 0))
+
+            @pl.when(c > 0)
+            def _():
+                finish_unit(0, h, c - 1)
+                finish_unit(1, h, c - 1)
+
+            return 0
+
+        lax.fori_loop(0, nc, body, 0)
+        finish_unit(0, h, nc - 1)
+        finish_unit(1, h, nc - 1)
+
+    own_tok.wait()
+    for copy in factors:
+        copy.wait()
+    low_of(gx)
+    gate_up(gx, True)
+
+    rb = 256
+
+    def norm_chunk(pairs, wcols, a_t, count):
+        def body(i, totals):
+            rows = pl.ds(pl.multiple_of(i * rb, rb), rb)
+            left = a_t[:, rows]
+            out = []
+            for (w, b), total in zip(pairs, totals):
+                merged = w[rows, wcols].astype(F32) + contract_first(left, b)
+                out.append(total + jnp.sum((merged * merged).reshape(rb // 8, 8, merged.shape[1]), axis=0))
+            return tuple(out)
+
+        zeros = tuple(jnp.zeros((8, b.shape[1]), F32) for _, b in pairs)
+        totals = lax.fori_loop(0, count // rb, body, zeros)
+        return [jnp.sum(total, axis=0, keepdims=True) for total in totals]
+
+    def only(value, n):
+        row = lax.broadcasted_iota(jnp.int32, value.shape, 0)
+        keep = jnp.logical_and(row >= n * rank, row < (n + 1) * rank)
+        return jnp.where(keep, value.astype(F32), 0.0).astype(BF16)
+
+    def gate_norms(c, _):
+        @pl.when(c + 2 < nc)
+        def _():
+            load_w(2, c + 2).start()
+
+        b = deep[:, cols(c)]
+        sums = norm_chunk(((wg, only(b, 0)), (wu, only(b, 1))), cols(c), wide, width)
+        ngs[gy, 0:1, cols(c)] = sums[0]
+        ngs[gy, 1:2, cols(c)] = sums[1]
+        return 0
+
+    lax.fori_loop(0, nc, gate_norms, 0)
+
+    def ng_copy(i):
+        peer = lax.rem(gy + i, 4)
+        return remote(ngs.at[gy], ngs.at[gy], ng_send.at[i - 1], ng_recv.at[gy], {"gy": peer})
+
+    for i in range(1, 4):
+        ng_copy(i).start()
+
+    pltpu.make_async_remote_copy(
+        src_ref=tok_hbm, dst_ref=xt.at[1 - gx], send_sem=in_send.at[0], recv_sem=in_recv.at[0],
+        device_id=y_peer, device_id_type=pl.DeviceIdType.MESH,
+    ).wait_recv()
+    low_of(1 - gx)
+    gate_up(1 - gx, False)
+    pl.semaphore_signal(credit.at[0], inc=1, device_id=core_peer, device_id_type=pl.DeviceIdType.MESH)
+
+    place = gx * 4 + gz
+    for c in range(nc):
+        load_w(2, c).wait()
+
+    def down_norms(t, _):
+        sums = norm_chunk(((wd, only(wide[:, tile(t)], 2)),), tile(t), deep, hidden_l)
+        nds[place, :, tile(t)] = sums[0]
+        return 0
+
+    lax.fori_loop(0, nt, down_norms, 0)
+
+    def group_copy(buf, i, send, recv):
+        peer, _ = group_peer(i)
+        return remote(buf.at[place], buf.at[place], send.at[i - 1], recv.at[place], peer)
+
+    def group_wait(buf, i, send, recv):
+        peer, src = group_peer(i)
+        remote(buf.at[src], buf.at[src], send.at[i - 1], recv.at[src], peer).wait_recv()
+
+    for i in range(1, 8):
+        group_copy(nds, i, nd_send, nd_recv.at[0]).start()
+    for i in range(1, 8):
+        group_wait(nds, i, nd_send, nd_recv.at[0])
+    total = nds[0]
+    for i in range(1, 8):
+        total = total + nds[i]
+    for i in range(width // LANES):
+        part_cols = slice(i * LANES, (i + 1) * LANES)
+        extra[1:2, part_cols] = m_d[i : i + 1]
+    scale_d = extra[1:2, 0:width] / jnp.sqrt(total + EPSILON)
+    own_cot.wait()
+    pltpu.make_async_remote_copy(
+        src_ref=cot_hbm, dst_ref=dl.at[1 - gx], send_sem=in_send.at[1], recv_sem=in_recv.at[1],
+        device_id=y_peer, device_id_type=pl.DeviceIdType.MESH,
+    ).wait_recv()
+    for h in range(2):
+        dl[h] = (dl[h].astype(F32) * scale_d).astype(BF16)
+
+    def rows2(ref, *idx):
+        value = ref[idx] if idx else ref[...]
+        return value.reshape(2 * half_t, value.shape[-1])
+
+    lane2 = lax.broadcasted_iota(jnp.int32, (2 * half_t, LANES), 1)
+    is_down = jnp.logical_and(lane2 >= 2 * rank, lane2 < 3 * rank)
+    down_back = jnp.where(is_down, contract_last(rows2(dl), wide[...]), 0.0)
+    la[0] = (rows2(low) + down_back).astype(BF16)
+    la_core = remote(la.at[0], lar.at[0], la_send.at[0], la_recv.at[0], core_peer)
+    la_core.start()
+    down_back = down_back.astype(BF16)
+
+    def hidden_grads(c, _):
+        value = contract_last(rows2(dl), wd[cols(c)]) + dot(down_back, deep[:, cols(c)])
+        for h in range(2):
+            slot = lax.rem(c, 2) * 2 + h
+            emit_unit(2, h, c, slot, value[h * half_t : (h + 1) * half_t], c >= 0)
+
+        @pl.when(c == 0)
+        def _():
+            la_core.wait_recv()
+            la[1] = (la[0].astype(F32) + lar[0].astype(F32)).astype(BF16)
+            remote(la.at[1], lar.at[1], la_send.at[1], la_recv.at[1], x_peer).start()
+
+        @pl.when(c > 0)
+        def _():
+            finish_unit(2, 0, c - 1)
+            finish_unit(2, 1, c - 1)
+
+        return 0
+
+    lax.fori_loop(0, nc, hidden_grads, 0)
+    finish_unit(2, 0, nc - 1)
+    finish_unit(2, 1, nc - 1)
+
+    for i in range(1, 4):
+        src = lax.rem(gy + i, 4)
+        remote(ngs.at[src], ngs.at[src], ng_send.at[i - 1], ng_recv.at[src], {"gy": src}).wait_recv()
+    for i in range(1, 4):
+        ng_copy(i).wait_send()
+    norm_gu = jnp.sqrt(ngs[0] + ngs[1] + ngs[2] + ngs[3] + EPSILON)
+    scale_gu[0] = norm_gu
+    for i in range(hidden_l // LANES):
+        part_cols = slice(i * LANES, (i + 1) * LANES)
+        for k in range(2):
+            scale_gu[1, k : k + 1, part_cols] = m_gu[k, i : i + 1] / norm_gu[k : k + 1, part_cols]
+
+    def ag_copy(k, buf, h, c):
+        return remote(
+            buf.at[h, mine, cols(c)], buf.at[h, mine, cols(c)],
+            ag_send.at[unit_id(k, h, c)], ag_recv.at[unit_id(k, h, c)], core_peer,
+        )
+
+    def ag_wait(k, buf, h, c):
+        remote(
+            buf.at[h, other_rows, cols(c)], buf.at[h, other_rows, cols(c)],
+            ag_send.at[unit_id(k, h, c)], ag_recv.at[unit_id(k, h, c)], core_peer,
+        ).wait_recv()
+
+    def lin(k, h, c):
+        return part[k, h, mine, cols(c)].astype(F32) + xr[k, h, :, cols(c)].astype(F32)
+
+    def hidden_of(h):
+        def body(c, _):
+            for k in range(2):
+                x_copy(k, h, c).wait()
+            gate_pre = lin(0, h, c) * scale_gu[1, 0:1, cols(c)]
+            up_pre = lin(1, h, c) * scale_gu[1, 1:2, cols(c)]
+            hid[h, mine, cols(c)] = (gate_pre * jax.nn.sigmoid(gate_pre) * up_pre).astype(BF16)
+            ag_copy(2, hid, h, c).start()
+            return 0
+
+        lax.fori_loop(0, nc, body, 0)
+
+    hidden_of(gx)
+    hidden_of(1 - gx)
+
+    def hidden_wait(c, _):
+        for h in range(2):
+            ag_wait(2, hid, h, c)
+            ag_copy(2, hid, h, c).wait_send()
+        return 0
+
+    lax.fori_loop(0, nc, hidden_wait, 0)
+
+    def low_chunk(c, total):
+        return total + contract_last(rows2(hid, slice(None), slice(None), cols(c)), deep[:, cols(c)])
+
+    down_low = lax.fori_loop(0, nc, low_chunk, jnp.zeros((2 * half_t, LANES), F32))
+    down_low = jnp.where(is_down, down_low, 0.0)
+    back[...] = down_low
+    down_low = down_low.astype(BF16)
+
+    sends = (
+        (lambda t: (ysend.at[:, tile(t)], yrecv.at[:, tile(t)], y_peer)),
+        (lambda t: (ykeep.at[pl.ds(pl.multiple_of((1 - bit0) * quarter, quarter), quarter), tile(t)], z1r.at[:, tile(t)], z1_peer)),
+        (lambda t: (z1r.at[pl.ds(pl.multiple_of((1 - bit1) * (quarter // 2), quarter // 2), quarter // 2), tile(t)], z2r.at[:, tile(t)], z2_peer)),
+    )
+    kept1 = pl.ds(pl.multiple_of(bit0 * quarter, quarter), quarter)
+    kept2 = pl.ds(pl.multiple_of(bit1 * (quarter // 2), quarter // 2), quarter // 2)
+    peer_block = pl.ds(pl.multiple_of((bit0 * 2 + 1 - bit1) * (quarter // 2), quarter // 2), quarter // 2)
+    gone1 = pl.ds(pl.multiple_of((1 - bit0) * quarter, quarter), quarter)
+
+    def yz(v, s, t):
+        if s < 3:
+            src, dst, peer = sends[s](t)
+        elif s == 3:
+            src, dst, peer = obuf.at[my_rows, tile(t)], obuf.at[my_rows, tile(t)], z2_peer
+        else:
+            src, dst, peer = obuf.at[kept1, tile(t)], obuf.at[kept1, tile(t)], z1_peer
+        return remote(src, dst, yz_send.at[v, s, t], yz_recv.at[v, s, t], peer)
+
+    def yz_wait(v, s, t):
+        if s < 3:
+            yz(v, s, t).wait_recv()
+        elif s == 3:
+            remote(obuf.at[my_rows, tile(t)], obuf.at[peer_block, tile(t)], yz_send.at[v, s, t], yz_recv.at[v, s, t], z2_peer).wait_recv()
+        else:
+            remote(obuf.at[kept1, tile(t)], obuf.at[gone1, tile(t)], yz_send.at[v, s, t], yz_recv.at[v, s, t], z1_peer).wait_recv()
+
+    def start_tile(v, t, value):
+        for h in range(2):
+            rows = value[h * half_t : (h + 1) * half_t].astype(BF16)
+
+            @pl.when(h == gx)
+            def _():
+                ykeep[:, tile(t)] = rows
+
+            @pl.when(h != gx)
+            def _():
+                ysend[:, tile(t)] = rows
+
+        yz(v, 0, t).start()
+
+    def yz_step(v, step):
+        def at(s):
+            t = step - s
+            return t, jnp.logical_and(t >= 0, t < nt)
+
+        t0, ok = at(0)
+
+        @pl.when(ok)
+        def _():
+            yz_wait(v, 0, t0)
+            total = ykeep[:, tile(t0)].astype(F32) + yrecv[:, tile(t0)].astype(F32)
+            ykeep[:, tile(t0)] = total.astype(BF16)
+            yz(v, 1, t0).start()
+
+        t1, ok = at(1)
+
+        @pl.when(ok)
+        def _():
+            yz_wait(v, 1, t1)
+            total = ykeep[kept1, tile(t1)].astype(F32) + z1r[:, tile(t1)].astype(F32)
+            z1r[:, tile(t1)] = total.astype(BF16)
+            yz(v, 2, t1).start()
+
+        t2, ok = at(2)
+
+        @pl.when(ok)
+        def _():
+            yz_wait(v, 2, t2)
+            total = z1r[kept2, tile(t2)].astype(F32) + z2r[:, tile(t2)].astype(F32)
+            if v == 0:
+                dots = cot_mine[:, tile(t2)].astype(F32) * total
+                gds[place, :, tile(t2)] = jnp.sum(dots, axis=0, keepdims=True)
+                total = total * scale_dv[:, tile(t2)]
+            obuf[my_rows, tile(t2)] = total.astype(BF16)
+            yz(v, 3, t2).start()
+
+        t3, ok = at(3)
+
+        @pl.when(ok)
+        def _():
+            yz_wait(v, 3, t3)
+            yz(v, 4, t3).start()
+
+        t4, ok = at(4)
+
+        @pl.when(ok)
+        def _():
+            yz_wait(v, 4, t4)
+            for s in range(5):
+                yz(v, s, t4).wait_send()
+
+    cot_rows.wait()
+    scale_dv = extra.at[0:1, 0:width]
+    scale_dv[...] = scale_d
+
+    def down_tile(t, _):
+        value = dot(rows2(hid), wd[:, tile(t)]) + dot(down_low, wide[:, tile(t)])
+        start_tile(0, t, value)
+        return 0
+
+    lax.fori_loop(0, nt, down_tile, 0)
+
+    acc[...] = jnp.zeros_like(acc)
+    pl.semaphore_wait(credit.at[0], 1)
+
+    def input_chunk(c):
+        for h in range(2):
+            ag_wait(0, part.at[0], h, c)
+            ag_wait(1, part.at[1], h, c)
+        gd = rows2(part, 0, slice(None), slice(None), cols(c))
+        ud = rows2(part, 1, slice(None), slice(None), cols(c))
+
+        def body(t, _):
+            acc[:, tile(t)] += contract_last(gd, wg[tile(t), cols(c)]) + contract_last(ud, wu[tile(t), cols(c)])
+            return 0
+
+        lax.fori_loop(0, nt, body, 0)
+        b = deep[:, cols(c)]
+        pair = jnp.where(lane2 < rank, contract_last(gd, b), contract_last(ud, b))
+        back[...] += jnp.where(lane2 < 2 * rank, pair, 0.0)
+
+    def grads(c, _):
+        sums = [None, None]
+        for h in range(2):
+            x_copy(2, h, c).wait()
+            s_g, s_u = scale_gu[1, 0:1, cols(c)], scale_gu[1, 1:2, cols(c)]
+            gate_lin, up_lin = lin(0, h, c), lin(1, h, c)
+            hgrad = lin(2, h, c).astype(BF16).astype(F32)
+            gate_pre, up_pre = gate_lin * s_g, up_lin * s_u
+            sig = jax.nn.sigmoid(gate_pre)
+            gate_grad = hgrad * up_pre * sig * (1.0 + gate_pre * (1.0 - sig))
+            up_grad = hgrad * (gate_pre * sig)
+            for k, value in ((0, gate_grad * gate_lin), (1, up_grad * up_lin)):
+                piece = jnp.sum(value, axis=0, keepdims=True)
+                sums[k] = piece if h == 0 else sums[k] + piece
+            part[0, h, mine, cols(c)] = (gate_grad * s_g).astype(BF16)
+            part[1, h, mine, cols(c)] = (up_grad * s_u).astype(BF16)
+            ag_copy(0, part.at[0], h, c).start()
+            ag_copy(1, part.at[1], h, c).start()
+        gms[0:1, cols(c)] = sums[0]
+        gms[1:2, cols(c)] = sums[1]
+
+        @pl.when(c > 0)
+        def _():
+            input_chunk(c - 1)
+
+        yz_step(0, c)
+        return 0
+
+    lax.fori_loop(0, nc, grads, 0)
+    gm_core = remote(gms, gmr, gm_sem.at[0], gm_sem.at[1], core_peer)
+    gm_core.start()
+    input_chunk(nc - 1)
+
+    def rest(step, _):
+        yz_step(0, step)
+        return 0
+
+    lax.fori_loop(nc, max(nc, nt + 4), rest, 0)
+    for n, peer in ((1, y_peer), (2, z1_peer), (3, z2_peer)):
+        pl.semaphore_signal(credit.at[n], inc=1, device_id=peer, device_id_type=pl.DeviceIdType.MESH)
+    for i in range(1, 8):
+        group_copy(gds, i, gd_send, nd_recv.at[1]).start()
+    for n in range(1, 4):
+        pl.semaphore_wait(credit.at[n], 1)
+    out_copy = pltpu.make_async_copy(obuf, out_hbm, out_sem.at[0])
+    out_copy.start()
+
+    back_gu = jnp.where(lane2 < 2 * rank, back[...], 0.0).astype(BF16)
+    lb[0] = back[...].astype(BF16)
+
+    def input_tile(t, _):
+        start_tile(1, t, acc[:, tile(t)] + dot(back_gu, wide[:, tile(t)]))
+        return 0
+
+    lax.fori_loop(0, nt, input_tile, 0)
+    lb_peers = (y_peer, z1_peer, z2_peer)
+
+    def lb_copy(n):
+        return remote(lb.at[n], lbr.at[n], lb_send.at[n], lb_recv.at[n], lb_peers[n])
+
+    lb_copy(0).start()
+    out_copy.wait()
+
+    def last(step, _):
+        yz_step(1, step)
+        for n in range(3):
+
+            @pl.when(step == nt - 1 + n)
+            def _():
+                lb_copy(n).wait()
+                lb[n + 1] = (lb[n].astype(F32) + lbr[n].astype(F32)).astype(BF16)
+                if n < 2:
+                    lb_copy(n + 1).start()
+
+        return 0
+
+    lax.fori_loop(0, nt + 4, last, 0)
+    gtok_copy = pltpu.make_async_copy(obuf, gtok_hbm, out_sem.at[1])
+    gtok_copy.start()
+
+    gm_core.wait()
+    gms[...] = (gms[...] + gmr[...]) / scale_gu[0]
+    for i in range(hidden_l // LANES):
+        for k in range(2):
+            gm_out[k, i : i + 1] = gms[k : k + 1, i * LANES : (i + 1) * LANES]
+    ends = [
+        pltpu.make_async_copy(gm_out.at[0], gmg_hbm, out_sem.at[2]),
+        pltpu.make_async_copy(gm_out.at[1], gmu_hbm, out_sem.at[3]),
+    ]
+    for i in range(1, 8):
+        group_wait(gds, i, gd_send, nd_recv.at[1])
+    for i in range(1, 8):
+        group_copy(gds, i, gd_send, nd_recv.at[1]).wait_send()
+        group_copy(nds, i, nd_send, nd_recv.at[0]).wait_send()
+    total, norm = gds[0], nds[0]
+    for i in range(1, 8):
+        total, norm = total + gds[i], norm + nds[i]
+    total = total / jnp.sqrt(norm + EPSILON)
+    for i in range(width // LANES):
+        gd_out[i : i + 1] = total[:, i * LANES : (i + 1) * LANES]
+    ends.append(pltpu.make_async_copy(gd_out, gdm_hbm, out_sem.at[4]))
+    for copy in ends:
+        copy.start()
+
+    la_core.wait_send()
+    remote(la.at[1], lar.at[1], la_send.at[1], la_recv.at[1], x_peer).wait()
+    la_t = (la[1].astype(F32) + lar[1].astype(F32)).T.astype(BF16)
+    lb_t = lb[3].astype(F32).T.astype(BF16)
+    acc[0 : 2 * rank] = dot(lb_t[: 2 * rank], rows2(xt))
+    acc[2 * rank : 3 * rank] = dot(lb_t[2 * rank : 3 * rank], rows2(dl))
+    for n, dst in enumerate((grg_hbm, gru_hbm, gde_hbm)):
+        ends.append(pltpu.make_async_copy(acc.at[n * rank : (n + 1) * rank], dst, out_sem.at[5 + n]))
+        ends[-1].start()
+    cut = hidden_l // 2
+    expand_outs = (geg_hbm, geu_hbm, gdr_hbm)
+    for k in range(3):
+        rows = la_t[k * rank : (k + 1) * rank]
+        for j in range(2):
+            piece = pl.ds(j * cut, cut)
+            if k < 2:
+                right = rows2(part, k, slice(None), slice(None), piece)
+            else:
+                right = rows2(hid, slice(None), slice(None), piece)
+            n = k * 2 + j
+            if n < 5:
+                where = acc.at[(3 + n) * rank : (4 + n) * rank, 0:cut]
+            else:
+                where = extra.at[:, 0:cut]
+            where[...] = dot(rows, right)
+            ends.append(pltpu.make_async_copy(where, expand_outs[k].at[:, piece], out_sem.at[8 + n]))
+            ends[-1].start()
+    for copy in ends + [gtok_copy]:
+        copy.wait()
+
+    send_tok.wait_send()
+    send_cot.wait_send()
+    for slot in range(4):
+        core_copy(2, slot % 2, nc - 1, slot).wait_send()
+
+    def ag_sends(c, _):
+        for h in range(2):
+            ag_copy(0, part.at[0], h, c).wait_send()
+            ag_copy(1, part.at[1], h, c).wait_send()
+        return 0
+
+    lax.fori_loop(0, nc, ag_sends, 0)
+
+
+def hand_over(*refs):
+    sources, targets, sem = refs[:11], refs[11:22], refs[22]
+    copies = [pltpu.make_async_copy(sources[i], targets[i], sem.at[i]) for i in range(11)]
+    for copy in copies:
+        copy.start()
+    for copy in copies:
+        copy.wait()
+
+
+def fits(tokens, gate_weight, gate_expand):
+    half_t, width = tokens.shape
+    hidden_l, rank = gate_weight.shape[1], gate_expand.shape[0]
+    sizes = tuple(lax.axis_size(name) for name in ("gx", "gy", "gz"))
+    return (
+        sizes == (2, 4, 4)
+        and 3 * rank <= LANES
+        and rank % 16 == 0
+        and half_t % 128 == 0
+        and width % LANES == 0
+        and 2 * half_t >= 8 * rank
+        and width % 256 == 0
+        and hidden_l % 512 == 0
+        and hidden_l % 256 == 0
+        and hidden_l >= 1024
+        and hidden_l // 2 <= width
+        and 6 * width * hidden_l <= 45 * 2**20
+        and half_t * width <= 2**18
+    )
+
+
+def fused(
+    tokens, cotangent, gate_weight, up_weight, down_weight, gate_reduce, gate_expand,
+    gate_magnitude, up_reduce, up_expand, up_magnitude, down_reduce, down_expand, down_magnitude,
+):
+    half_t, width = tokens.shape
+    hidden_l, rank = gate_weight.shape[1], gate_expand.shape[0]
+    all_t, quarter = 2 * half_t, half_t // 2
+    fc, dt = 512, 512 if width % 512 == 0 else width
+    nc, nt = hidden_l // fc, width // dt
+    any_space = pl.BlockSpec(memory_space=pl.ANY)
+    dma = pltpu.SemaphoreType.DMA
+    units = 6 * nc
+    rows_f, rows_d = hidden_l // LANES, width // LANES
+    shapes = (
+        ((half_t, width), BF16), ((half_t, width), BF16),
+        ((rank, width), F32), ((rank, width), F32), ((rank, width), F32),
+        ((rank, hidden_l), F32), ((rank, hidden_l), F32), ((rank, hidden_l), F32),
+        ((rows_f, LANES), F32), ((rows_f, LANES), F32), ((rows_d, LANES), F32),
+    )
+    results = pl.pallas_call(
+        kernel,
+        out_shape=[jax.ShapeDtypeStruct(*pair) for pair in shapes],
+        in_specs=[any_space] * 14,
+        out_specs=[any_space] * 11,
+        scratch_shapes=[
+            pltpu.VMEM((LANES, width), BF16),
+            pltpu.VMEM((LANES, hidden_l), BF16),
+            pltpu.VMEM((2, rows_f, LANES), F32),
+            pltpu.VMEM((rows_d, LANES), F32),
+            pltpu.VMEM((2, rows_f, LANES), F32),
+            pltpu.VMEM((rows_d, LANES), F32),
+            pltpu.VMEM((width, hidden_l), BF16),
+            pltpu.VMEM((width, hidden_l), BF16),
+            pltpu.VMEM((hidden_l, width), BF16),
+            pltpu.VMEM((2, half_t, width), BF16),
+            pltpu.VMEM((2, half_t, width), BF16),
+            pltpu.VMEM((3, 2, half_t, hidden_l), BF16),
+            pltpu.VMEM((3, 2, quarter, hidden_l), BF16),
+            pltpu.VMEM((2, half_t, hidden_l), BF16),
+            pltpu.VMEM((4, quarter, fc), BF16),
+            pltpu.VMEM((all_t, width), F32),
+            pltpu.VMEM((half_t, width), BF16),
+            pltpu.VMEM((half_t, width), BF16),
+            pltpu.VMEM((half_t, width), BF16),
+            pltpu.VMEM((quarter, width), BF16),
+            pltpu.VMEM((quarter // 2, width), BF16),
+            pltpu.VMEM((half_t, width), BF16),
+            pltpu.VMEM((half_t // 4, width), BF16),
+            pltpu.VMEM((2, half_t, LANES), F32),
+            pltpu.VMEM((2, all_t, LANES), BF16),
+            pltpu.VMEM((2, all_t, LANES), BF16),
+            pltpu.VMEM((all_t, LANES), F32),
+            pltpu.VMEM((4, all_t, LANES), BF16),
+            pltpu.VMEM((3, all_t, LANES), BF16),
+            pltpu.VMEM((8, 1, width), F32),
+            pltpu.VMEM((4, 2, hidden_l), F32),
+            pltpu.VMEM((2, 2, hidden_l), F32),
+            pltpu.VMEM((2, hidden_l), F32),
+            pltpu.VMEM((2, hidden_l), F32),
+            pltpu.VMEM((8, 1, width), F32),
+            pltpu.VMEM((rank, width), F32),
+            dma((3, nc)),
+            dma((12,)),
+            dma((2,)),
+            dma((2,)),
+            dma((4,)),
+            dma((units,)),
+            dma((units,)),
+            dma((units,)),
+            dma((units,)),
+            dma((units,)),
+            dma((2, 5, nt)),
+            dma((2, 5, nt)),
+            dma((7,)),
+            dma((7,)),
+            dma((2, 8)),
+            dma((3,)),
+            dma((4,)),
+            dma((2,)),
+            dma((2,)),
+            dma((3,)),
+            dma((3,)),
+            dma((2,)),
+            dma((14,)),
+            pltpu.SemaphoreType.REGULAR((4,)),
+        ],
+        compiler_params=pltpu.CompilerParams(
+            collective_id=0, has_side_effects=True, vmem_limit_bytes=67043328
+        ),
+    )(
+        tokens, cotangent, gate_weight, up_weight, down_weight, gate_reduce.T, up_reduce.T,
+        down_expand, gate_expand, up_expand, down_reduce.T, gate_magnitude.reshape(rows_f, LANES),
+        up_magnitude.reshape(rows_f, LANES), down_magnitude.reshape(rows_d, LANES),
+    )
+    results = pl.pallas_call(
+        hand_over,
+        out_shape=[jax.ShapeDtypeStruct(*pair) for pair in shapes],
+        in_specs=[pl.BlockSpec(memory_space=pltpu.VMEM)] * 11,
+        out_specs=[any_space] * 11,
+        scratch_shapes=[dma((11,))],
+        compiler_params=pltpu.CompilerParams(vmem_limit_bytes=2**23),
+    )(*results)
+    output, grad_tokens, grg, gru, gde, geg, geu, gdr, gmg, gmu, gdm = results
+    return (
+        output, grad_tokens, grg.T, geg, gmg.reshape(-1), gru.T, geu, gmu.reshape(-1),
+        gdr.T, gde, gdm.reshape(-1),
+    )
+
+
+def choose_body(mesh):
+    def body(*args):
+        if fits(args[0], args[2], args[6]):
+            return fused(*args)
+        return on_device(*args)
+
+    return body
+
+
 def solution(mesh):
     return jax.shard_map(
-        on_device,
+        choose_body(mesh),
         mesh=mesh,
         in_specs=(
             P("gx", "gy"),

time: 486 us -> 158 us (0.33)
  waiting for transfers between devices: 231 us -> 0 us
  Pallas kernels: 0 us -> 146 us
  matrix products: 116 us -> 0 us
  blocking collectives: 106 us -> 0 us
  between operations: 14.3 us -> 0.68 us
  other arithmetic: 8.95 us -> 0 us
    pallas_call x0 -> x2, Pallas kernels: none -> 146 us  [the longest x1 144 us: fused(): pl.pallas_call(kernel, out_shape=[jax.ShapeDtypeStruct(*pair) for pair in...]
    dot_general x27 -> x0, matrix products: 116 us -> none  [the longest x9 44.7 us: contract_last(): lax.dot_general(left, right, (((1,), (1,)), ((), ())), preferred_element_...]
    reduce_scatter x5 -> x0, waiting for transfers between devices: 101 us -> none  [scatter_pair(): summed = lax.psum_scatter(joined, axes, scatter_dimension=0, tiled=True)]
    all_gather x5 -> x0, waiting for transfers between devices: 90.5 us -> none  [the longest x1 21 us: on_device(): all_hidden = lax.all_gather(hidden, 'gy', axis=0, tiled=True)]
    psum x4 -> x0, blocking collectives: 66.4 us -> none  [the longest x1 23.7 us: on_device(): norm_down = jnp.sqrt(lax.psum(square_down, ('gx', 'gz')) + EPSILON)]
    all_gather x3 -> x0, blocking collectives: 39.5 us -> none  [the longest x1 17.7 us: on_device(): lax.all_gather((down_lin * scale_down[None, :]).astype(jnp.bfloat16), 'gz...]
    psum x1 -> x0, waiting for transfers between devices: 37.6 us -> none  [on_device(): lax.psum((grad_gate_reduce, grad_up_reduce), ('gx', 'gz'))]
    unnamed x59 -> x22, local copies, waits for them, and re-layouts: 3.95 us -> 10.1 us
  transfers between devices with their start and end apart: 11 -> 0, of which waited for: 10 -> 0; matrix products, arithmetic and copies ran while one was open for 21% -> 0% of each run, Pallas kernels for 0% -> 0%
where the time goes in v1:
time: 158 us; the launch traced here: 157 us
  Pallas kernels  146 us (92%)
  local copies, waits for them, and re-layouts  10.1 us (6%)
    pallas_call x1, Pallas kernels, fused(): pl.pallas_call(kernel, out_shape=[jax.ShapeDtypeStruct(*pair) for pair in...  144 us
    unnamed x22, local copies, waits for them, and re-layouts  10.1 us

profile of v1, /device:TPU:0, one launch (start us, length us, event | category | flops | bytes accessed | tf_op | source)
XLA Modules:
  0.0 157.0 jit_solution(10040545721000476632)
XLA Ops:
  0.6 144.5 %shard_map.221 = (bf16[128,2048]{1,0:T(8,128)(2,1)}, bf16[128,2048]{1,0:T(8,128)(2,1)}, f32[32,2048]{1,0:T(8,128)}, f32[32,2048]{1,0:T(8,128)}, f32[32,2048]{1,0...) custom-call(bf16[128,2048]{1,0:T(8,128)(2,1)} %tok_hbm.1, ...), custom_call_target="tpu_custom_call" | custom-call | tf_op jit(solution)/shard_map/pallas_call | solution.py:851
  145.1 0.0 copy-start
  145.1 1.0 copy-done
  146.2 0.0 copy-start.1
  146.2 1.0 copy-done.1
  147.2 0.0 copy-start.2
  147.2 1.0 copy-done.2
  148.2 0.0 copy-start.3
  148.2 1.0 copy-done.3
  149.2 0.0 copy-start.4
  149.3 1.0 copy-done.4
  150.3 0.0 copy-start.5
  150.3 0.9 copy-done.5
  151.2 0.0 copy-start.6
  151.2 0.9 copy-done.6
  152.2 0.0 copy-start.7
  152.2 0.9 copy-done.7
  153.1 0.0 copy-start.8
  153.1 0.7 copy-done.8
  153.8 0.0 copy-start.9
  153.8 0.7 copy-done.9
  154.6 0.0 copy-start.10
  154.6 0.7 copy-done.10
  155.3 1.8 %shard_map.222 = (bf16[128,2048]{1,0:T(8,128)(2,1)}, bf16[128,2048]{1,0:T(8,128)(2,1)}, f32[32,2048]{1,0:T(8,128)}, f32[32,2048]{1,0:T(8,128)}, f32[32,2048]{1,0...) custom-call(bf16[128,2048]{1,0:T(8,128)(2,1)S(1)} %copy-done, ...), custom_call_target="tpu_custom_call" | custom-call | tf_op jit(solution)/shard_map/pallas_call | solution.py:926
Async XLA Ops:
  145.1 1.0 copy-start
  146.2 1.0 copy-start.1
  147.2 1.0 copy-start.2
  148.2 1.0 copy-start.3
  149.2 1.0 copy-start.4
  150.3 0.9 copy-start.5
  151.2 0.9 copy-start.6
  152.2 0.9 copy-start.7
  153.1 0.7 copy-start.8
  153.8 0.7 copy-start.9
  154.6 0.7 copy-start.10

commit v2 on v1

--- a/solution.py
+++ b/solution.py
@@ -196,7 +196,7 @@
     rank = gde_hbm.shape[0]
     fc = cs.shape[2]
     nc = hidden_l // fc
-    dt = 512 if width % 512 == 0 else width
+    dt = 256
     nt = width // dt
     mine = pl.ds(pl.multiple_of(core * quarter, quarter), quarter)
 
@@ -260,7 +260,6 @@
     send_tok = remote(tok_hbm, xt.at[gx], in_send.at[0], in_recv.at[0], y_peer)
     send_cot = remote(cot_hbm, dl.at[gx], in_send.at[1], in_recv.at[1], y_peer)
     send_tok.start()
-    send_cot.start()
     own_cot.start()
     cot_rows.start()
 
@@ -308,6 +307,19 @@
         part[k, h, mine, cols(c)] = total.astype(BF16)
         x_copy(k, h, c).start()
 
+    rb = 256
+
+    def squares(w, wcols, count):
+        total = None
+        for i in range(count // rb):
+            piece = w[i * rb : (i + 1) * rb, wcols].astype(F32)
+            piece = jnp.sum((piece * piece).reshape(rb // 8, 8, piece.shape[1]), axis=0)
+            total = piece if total is None else total + piece
+        return jnp.sum(total, axis=0, keepdims=True)
+
+    def fold(factor, cross, spread):
+        return jnp.sum(factor * (2.0 * cross + spread), axis=0, keepdims=True)
+
     def gate_up(h, first):
         x_low = low[h]
         low_gate = jnp.where(is_gate, x_low, 0.0).astype(BF16)
@@ -327,8 +339,22 @@
                 def _():
                     load_w(2, c + 2 - nc).start()
 
+            if first:
+                factor = deep[0 : 2 * rank, cols(c)]
+                spread = dot(gram_hi, factor) + dot(gram_lo, factor)
+                factor = factor.astype(F32)
             for k, w, lw in ((0, wg, low_gate), (1, wu, low_up)):
-                value = dot(xt[h], w[:, cols(c)]) + dot(lw, deep[:, cols(c)])
+                extra_value = dot(lw, deep[:, cols(c)])
+                if first:
+                    left = jnp.concatenate([xt[h], wide[0 : 2 * rank]], axis=0)
+                    both = dot(left, w[:, cols(c)])
+                    value = both[:half_t] + extra_value
+                    mine_rows = slice(k * rank, (k + 1) * rank)
+                    ngs[gy, k : k + 1, cols(c)] = squares(w, cols(c), width) + fold(
+                        factor[mine_rows], both[half_t:][mine_rows], spread[mine_rows]
+                    )
+                else:
+                    value = dot(xt[h], w[:, cols(c)]) + extra_value
                 slot = lax.rem(c, 2) * 2 + k
                 emit_unit(k, h, c, slot, value, (c >= 2) if first else (c >= 0))
 
@@ -347,41 +373,16 @@
     for copy in factors:
         copy.wait()
     low_of(gx)
+    gram = contract_last(wide[0 : 2 * rank], wide[0 : 2 * rank])
+    side = lax.broadcasted_iota(jnp.int32, gram.shape, 0) < rank
+    side = side == (lax.broadcasted_iota(jnp.int32, gram.shape, 1) < rank)
+    gram = jnp.where(side, gram, 0.0)
+    gram_hi = gram.astype(BF16)
+    gram_lo = (gram - gram_hi.astype(F32)).astype(BF16)
     gate_up(gx, True)
 
-    rb = 256
-
-    def norm_chunk(pairs, wcols, a_t, count):
-        def body(i, totals):
-            rows = pl.ds(pl.multiple_of(i * rb, rb), rb)
-            left = a_t[:, rows]
-            out = []
-            for (w, b), total in zip(pairs, totals):
-                merged = w[rows, wcols].astype(F32) + contract_first(left, b)
-                out.append(total + jnp.sum((merged * merged).reshape(rb // 8, 8, merged.shape[1]), axis=0))
-            return tuple(out)
-
-        zeros = tuple(jnp.zeros((8, b.shape[1]), F32) for _, b in pairs)
-        totals = lax.fori_loop(0, count // rb, body, zeros)
-        return [jnp.sum(total, axis=0, keepdims=True) for total in totals]
-
-    def only(value, n):
-        row = lax.broadcasted_iota(jnp.int32, value.shape, 0)
-        keep = jnp.logical_and(row >= n * rank, row < (n + 1) * rank)
-        return jnp.where(keep, value.astype(F32), 0.0).astype(BF16)
-
-    def gate_norms(c, _):
-        @pl.when(c + 2 < nc)
-        def _():
-            load_w(2, c + 2).start()
-
-        b = deep[:, cols(c)]
-        sums = norm_chunk(((wg, only(b, 0)), (wu, only(b, 1))), cols(c), wide, width)
-        ngs[gy, 0:1, cols(c)] = sums[0]
-        ngs[gy, 1:2, cols(c)] = sums[1]
-        return 0
-
-    lax.fori_loop(0, nc, gate_norms, 0)
+    for c in range(2, nc):
+        load_w(2, c).start()
 
     def ng_copy(i):
         peer = lax.rem(gy + i, 4)
@@ -390,6 +391,37 @@
     for i in range(1, 4):
         ng_copy(i).start()
 
+    send_tok.wait_send()
+    send_cot.start()
+
+    place = gx * 4 + gz
+    for c in range(nc):
+        load_w(2, c).wait()
+
+    down_in = slice(2 * rank, 3 * rank)
+    gram_d = contract_last(deep[down_in], deep[down_in])
+    gram_d_hi = gram_d.astype(BF16)
+    gram_d_lo = (gram_d - gram_d_hi.astype(F32)).astype(BF16)
+
+    def down_norms(t, _):
+        factor = wide[down_in, tile(t)]
+        spread = dot(gram_d_hi, factor) + dot(gram_d_lo, factor)
+        cross = dot(deep[down_in], wd[:, tile(t)])
+        nds[place, :, tile(t)] = squares(wd, tile(t), hidden_l) + fold(factor.astype(F32), cross, spread)
+        return 0
+
+    lax.fori_loop(0, nt, down_norms, 0)
+
+    def group_copy(buf, i, send, recv):
+        peer, _ = group_peer(i)
+        return remote(buf.at[place], buf.at[place], send.at[i - 1], recv.at[place], peer)
+
+    def group_wait(buf, i, send, recv):
+        peer, src = group_peer(i)
+        remote(buf.at[src], buf.at[src], send.at[i - 1], recv.at[src], peer).wait_recv()
+
+    for i in range(1, 8):
+        group_copy(nds, i, nd_send, nd_recv.at[0]).start()
     pltpu.make_async_remote_copy(
         src_ref=tok_hbm, dst_ref=xt.at[1 - gx], send_sem=in_send.at[0], recv_sem=in_recv.at[0],
         device_id=y_peer, device_id_type=pl.DeviceIdType.MESH,
@@ -398,27 +430,6 @@
     gate_up(1 - gx, False)
     pl.semaphore_signal(credit.at[0], inc=1, device_id=core_peer, device_id_type=pl.DeviceIdType.MESH)
 
-    place = gx * 4 + gz
-    for c in range(nc):
-        load_w(2, c).wait()
-
-    def down_norms(t, _):
-        sums = norm_chunk(((wd, only(wide[:, tile(t)], 2)),), tile(t), deep, hidden_l)
-        nds[place, :, tile(t)] = sums[0]
-        return 0
-
-    lax.fori_loop(0, nt, down_norms, 0)
-
-    def group_copy(buf, i, send, recv):
-        peer, _ = group_peer(i)
-        return remote(buf.at[place], buf.at[place], send.at[i - 1], recv.at[place], peer)
-
-    def group_wait(buf, i, send, recv):
-        peer, src = group_peer(i)
-        remote(buf.at[src], buf.at[src], send.at[i - 1], recv.at[src], peer).wait_recv()
-
-    for i in range(1, 8):
-        group_copy(nds, i, nd_send, nd_recv.at[0]).start()
     for i in range(1, 8):
         group_wait(nds, i, nd_send, nd_recv.at[0])
     total = nds[0]
@@ -427,7 +438,7 @@
     for i in range(width // LANES):
         part_cols = slice(i * LANES, (i + 1) * LANES)
         extra[1:2, part_cols] = m_d[i : i + 1]
-    scale_d = extra[1:2, 0:width] / jnp.sqrt(total + EPSILON)
+    scale_d = extra[1:2, 0:width] / jnp.sqrt(jnp.maximum(total, 0.0) + EPSILON)
     own_cot.wait()
     pltpu.make_async_remote_copy(
         src_ref=cot_hbm, dst_ref=dl.at[1 - gx], send_sem=in_send.at[1], recv_sem=in_recv.at[1],
@@ -476,7 +487,7 @@
         remote(ngs.at[src], ngs.at[src], ng_send.at[i - 1], ng_recv.at[src], {"gy": src}).wait_recv()
     for i in range(1, 4):
         ng_copy(i).wait_send()
-    norm_gu = jnp.sqrt(ngs[0] + ngs[1] + ngs[2] + ngs[3] + EPSILON)
+    norm_gu = jnp.sqrt(jnp.maximum(ngs[0] + ngs[1] + ngs[2] + ngs[3], 0.0) + EPSILON)
     scale_gu[0] = norm_gu
     for i in range(hidden_l // LANES):
         part_cols = slice(i * LANES, (i + 1) * LANES)
@@ -570,56 +581,35 @@
 
         yz(v, 0, t).start()
 
-    def yz_step(v, step):
-        def at(s):
-            t = step - s
-            return t, jnp.logical_and(t >= 0, t < nt)
-
-        t0, ok = at(0)
-
-        @pl.when(ok)
-        def _():
-            yz_wait(v, 0, t0)
-            total = ykeep[:, tile(t0)].astype(F32) + yrecv[:, tile(t0)].astype(F32)
-            ykeep[:, tile(t0)] = total.astype(BF16)
-            yz(v, 1, t0).start()
-
-        t1, ok = at(1)
-
-        @pl.when(ok)
-        def _():
-            yz_wait(v, 1, t1)
-            total = ykeep[kept1, tile(t1)].astype(F32) + z1r[:, tile(t1)].astype(F32)
-            z1r[:, tile(t1)] = total.astype(BF16)
-            yz(v, 2, t1).start()
-
-        t2, ok = at(2)
-
-        @pl.when(ok)
-        def _():
-            yz_wait(v, 2, t2)
-            total = z1r[kept2, tile(t2)].astype(F32) + z2r[:, tile(t2)].astype(F32)
+    def yz_stage(v, s, t):
+        yz_wait(v, s, t)
+        if s == 0:
+            total = ykeep[:, tile(t)].astype(F32) + yrecv[:, tile(t)].astype(F32)
+            ykeep[:, tile(t)] = total.astype(BF16)
+        elif s == 1:
+            total = ykeep[kept1, tile(t)].astype(F32) + z1r[:, tile(t)].astype(F32)
+            z1r[:, tile(t)] = total.astype(BF16)
+        elif s == 2:
+            total = z1r[kept2, tile(t)].astype(F32) + z2r[:, tile(t)].astype(F32)
             if v == 0:
-                dots = cot_mine[:, tile(t2)].astype(F32) * total
-                gds[place, :, tile(t2)] = jnp.sum(dots, axis=0, keepdims=True)
-                total = total * scale_dv[:, tile(t2)]
-            obuf[my_rows, tile(t2)] = total.astype(BF16)
-            yz(v, 3, t2).start()
-
-        t3, ok = at(3)
-
-        @pl.when(ok)
-        def _():
-            yz_wait(v, 3, t3)
-            yz(v, 4, t3).start()
-
-        t4, ok = at(4)
-
-        @pl.when(ok)
-        def _():
-            yz_wait(v, 4, t4)
-            for s in range(5):
-                yz(v, s, t4).wait_send()
+                dots = cot_mine[:, tile(t)].astype(F32) * total
+                gds[place, :, tile(t)] = jnp.sum(dots, axis=0, keepdims=True)
+                total = total * scale_dv[:, tile(t)]
+            obuf[my_rows, tile(t)] = total.astype(BF16)
+        if s < 4:
+            yz(v, s + 1, t).start()
+        else:
+            for n in range(5):
+                yz(v, n, t).wait_send()
+
+    def yz_step(v, step, group, spacing):
+        for s in range(5):
+            t = step - spacing * s
+
+            @pl.when(jnp.logical_and(t >= 0, t < nt // group))
+            def _():
+                for n in range(group):
+                    yz_stage(v, s, t * group + n)
 
     cot_rows.wait()
     scale_dv = extra.at[0:1, 0:width]
@@ -635,21 +625,38 @@
     acc[...] = jnp.zeros_like(acc)
     pl.semaphore_wait(credit.at[0], 1)
 
-    def input_chunk(c):
+    def input_chunk(c, closing=False):
         for h in range(2):
             ag_wait(0, part.at[0], h, c)
             ag_wait(1, part.at[1], h, c)
         gd = rows2(part, 0, slice(None), slice(None), cols(c))
         ud = rows2(part, 1, slice(None), slice(None), cols(c))
 
-        def body(t, _):
-            acc[:, tile(t)] += contract_last(gd, wg[tile(t), cols(c)]) + contract_last(ud, wu[tile(t), cols(c)])
-            return 0
-
-        lax.fori_loop(0, nt, body, 0)
         b = deep[:, cols(c)]
         pair = jnp.where(lane2 < rank, contract_last(gd, b), contract_last(ud, b))
         back[...] += jnp.where(lane2 < 2 * rank, pair, 0.0)
+
+        def piece(t):
+            return contract_last(gd, wg[tile(t), cols(c)]) + contract_last(ud, wu[tile(t), cols(c)])
+
+        if not closing:
+
+            def body(t, _):
+                acc[:, tile(t)] += piece(t)
+                return 0
+
+            lax.fori_loop(0, nt, body, 0)
+            return
+        lb[0] = back[...].astype(BF16)
+        back_gu = jnp.where(lane2 < 2 * rank, back[...], 0.0).astype(BF16)
+        for n in range(1, 4):
+            pl.semaphore_wait(credit.at[n], 1)
+
+        def input_tile(t, _):
+            start_tile(1, t, acc[:, tile(t)] + piece(t) + dot(back_gu, wide[:, tile(t)]))
+            return 0
+
+        lax.fori_loop(0, nt, input_tile, 0)
 
     def grads(c, _):
         sums = [None, None]
@@ -676,36 +683,26 @@
         def _():
             input_chunk(c - 1)
 
-        yz_step(0, c)
+        yz_step(0, c, 2, 1)
         return 0
 
     lax.fori_loop(0, nc, grads, 0)
     gm_core = remote(gms, gmr, gm_sem.at[0], gm_sem.at[1], core_peer)
     gm_core.start()
-    input_chunk(nc - 1)
 
     def rest(step, _):
-        yz_step(0, step)
+        yz_step(0, step, 2, 1)
         return 0
 
-    lax.fori_loop(nc, max(nc, nt + 4), rest, 0)
+    lax.fori_loop(nc, max(nc, nt // 2 + 4), rest, 0)
     for n, peer in ((1, y_peer), (2, z1_peer), (3, z2_peer)):
         pl.semaphore_signal(credit.at[n], inc=1, device_id=peer, device_id_type=pl.DeviceIdType.MESH)
     for i in range(1, 8):
         group_copy(gds, i, gd_send, nd_recv.at[1]).start()
-    for n in range(1, 4):
-        pl.semaphore_wait(credit.at[n], 1)
     out_copy = pltpu.make_async_copy(obuf, out_hbm, out_sem.at[0])
     out_copy.start()
 
-    back_gu = jnp.where(lane2 < 2 * rank, back[...], 0.0).astype(BF16)
-    lb[0] = back[...].astype(BF16)
-
-    def input_tile(t, _):
-        start_tile(1, t, acc[:, tile(t)] + dot(back_gu, wide[:, tile(t)]))
-        return 0
-
-    lax.fori_loop(0, nt, input_tile, 0)
+    input_chunk(nc - 1, closing=True)
     lb_peers = (y_peer, z1_peer, z2_peer)
 
     def lb_copy(n):
@@ -713,57 +710,11 @@
 
     lb_copy(0).start()
     out_copy.wait()
-
-    def last(step, _):
-        yz_step(1, step)
-        for n in range(3):
-
-            @pl.when(step == nt - 1 + n)
-            def _():
-                lb_copy(n).wait()
-                lb[n + 1] = (lb[n].astype(F32) + lbr[n].astype(F32)).astype(BF16)
-                if n < 2:
-                    lb_copy(n + 1).start()
-
-        return 0
-
-    lax.fori_loop(0, nt + 4, last, 0)
-    gtok_copy = pltpu.make_async_copy(obuf, gtok_hbm, out_sem.at[1])
-    gtok_copy.start()
-
-    gm_core.wait()
-    gms[...] = (gms[...] + gmr[...]) / scale_gu[0]
-    for i in range(hidden_l // LANES):
-        for k in range(2):
-            gm_out[k, i : i + 1] = gms[k : k + 1, i * LANES : (i + 1) * LANES]
-    ends = [
-        pltpu.make_async_copy(gm_out.at[0], gmg_hbm, out_sem.at[2]),
-        pltpu.make_async_copy(gm_out.at[1], gmu_hbm, out_sem.at[3]),
-    ]
-    for i in range(1, 8):
-        group_wait(gds, i, gd_send, nd_recv.at[1])
-    for i in range(1, 8):
-        group_copy(gds, i, gd_send, nd_recv.at[1]).wait_send()
-        group_copy(nds, i, nd_send, nd_recv.at[0]).wait_send()
-    total, norm = gds[0], nds[0]
-    for i in range(1, 8):
-        total, norm = total + gds[i], norm + nds[i]
-    total = total / jnp.sqrt(norm + EPSILON)
-    for i in range(width // LANES):
-        gd_out[i : i + 1] = total[:, i * LANES : (i + 1) * LANES]
-    ends.append(pltpu.make_async_copy(gd_out, gdm_hbm, out_sem.at[4]))
-    for copy in ends:
-        copy.start()
 
     la_core.wait_send()
     remote(la.at[1], lar.at[1], la_send.at[1], la_recv.at[1], x_peer).wait()
     la_t = (la[1].astype(F32) + lar[1].astype(F32)).T.astype(BF16)
-    lb_t = lb[3].astype(F32).T.astype(BF16)
-    acc[0 : 2 * rank] = dot(lb_t[: 2 * rank], rows2(xt))
-    acc[2 * rank : 3 * rank] = dot(lb_t[2 * rank : 3 * rank], rows2(dl))
-    for n, dst in enumerate((grg_hbm, gru_hbm, gde_hbm)):
-        ends.append(pltpu.make_async_copy(acc.at[n * rank : (n + 1) * rank], dst, out_sem.at[5 + n]))
-        ends[-1].start()
+    ends = []
     cut = hidden_l // 2
     expand_outs = (geg_hbm, geu_hbm, gdr_hbm)
     for k in range(3):
@@ -782,10 +733,59 @@
             where[...] = dot(rows, right)
             ends.append(pltpu.make_async_copy(where, expand_outs[k].at[:, piece], out_sem.at[8 + n]))
             ends[-1].start()
-    for copy in ends + [gtok_copy]:
+    low_ends = [
+        pltpu.make_async_copy(acc.at[n * rank : (n + 1) * rank], dst, out_sem.at[5 + n])
+        for n, dst in enumerate((grg_hbm, gru_hbm, gde_hbm))
+    ]
+
+    gm_core.wait()
+    gms[...] = (gms[...] + gmr[...]) / scale_gu[0]
+    for i in range(hidden_l // LANES):
+        for k in range(2):
+            gm_out[k, i : i + 1] = gms[k : k + 1, i * LANES : (i + 1) * LANES]
+    for i in range(1, 8):
+        group_wait(gds, i, gd_send, nd_recv.at[1])
+    for i in range(1, 8):
+        group_copy(gds, i, gd_send, nd_recv.at[1]).wait_send()
+        group_copy(nds, i, nd_send, nd_recv.at[0]).wait_send()
+    total, norm = gds[0], nds[0]
+    for i in range(1, 8):
+        total, norm = total + gds[i], norm + nds[i]
+    total = total / jnp.sqrt(jnp.maximum(norm, 0.0) + EPSILON)
+    for i in range(width // LANES):
+        gd_out[i : i + 1] = total[:, i * LANES : (i + 1) * LANES]
+    for i, (src, dst) in enumerate(((gm_out.at[0], gmg_hbm), (gm_out.at[1], gmu_hbm), (gd_out, gdm_hbm))):
+        ends.append(pltpu.make_async_copy(src, dst, out_sem.at[2 + i]))
+        ends[-1].start()
+
+    def last(step, _):
+        @pl.when(step == nt + 7)
+        def _():
+            lb_t = lb[3].astype(F32).T.astype(BF16)
+            acc[0 : 2 * rank] = dot(lb_t[: 2 * rank], rows2(xt))
+            acc[2 * rank : 3 * rank] = dot(lb_t[2 * rank : 3 * rank], rows2(dl))
+            for copy in low_ends:
+                copy.start()
+
+        yz_step(1, step, 1, 2)
+        for n in range(3):
+
+            @pl.when(step == nt + 1 + 2 * n)
+            def _():
+                lb_copy(n).wait()
+                lb[n + 1] = (lb[n].astype(F32) + lbr[n].astype(F32)).astype(BF16)
+                if n < 2:
+                    lb_copy(n + 1).start()
+
+        return 0
+
+    lax.fori_loop(0, nt + 8, last, 0)
+    gtok_copy = pltpu.make_async_copy(obuf, gtok_hbm, out_sem.at[1])
+    gtok_copy.start()
+
+    for copy in ends + low_ends + [gtok_copy]:
         copy.wait()
 
-    send_tok.wait_send()
     send_cot.wait_send()
     for slot in range(4):
         core_copy(2, slot % 2, nc - 1, slot).wait_send()
@@ -800,11 +800,16 @@
 
 
 def hand_over(*refs):
-    sources, targets, sem = refs[:11], refs[11:22], refs[22]
-    copies = [pltpu.make_async_copy(sources[i], targets[i], sem.at[i]) for i in range(11)]
-    for copy in copies:
+    sources, targets, stops = refs[:11], refs[11:22], refs[22:33]
+    in_sem, out_sem = refs[33:]
+    reads = [pltpu.make_async_copy(sources[i], stops[i], in_sem.at[i]) for i in range(11)]
+    writes = [pltpu.make_async_copy(stops[i], targets[i], out_sem.at[i]) for i in range(11)]
+    for copy in reads:
         copy.start()
-    for copy in copies:
+    for read, write in zip(reads, writes):
+        read.wait()
+        write.start()
+    for copy in writes:
         copy.wait()
 
 
@@ -819,7 +824,7 @@
         and half_t % 128 == 0
         and width % LANES == 0
         and 2 * half_t >= 8 * rank
-        and width % 256 == 0
+        and width % 512 == 0
         and hidden_l % 512 == 0
         and hidden_l % 256 == 0
         and hidden_l >= 1024
@@ -836,7 +841,7 @@
     half_t, width = tokens.shape
     hidden_l, rank = gate_weight.shape[1], gate_expand.shape[0]
     all_t, quarter = 2 * half_t, half_t // 2
-    fc, dt = 512, 512 if width % 512 == 0 else width
+    fc, dt = 512, 256
     nc, nt = hidden_l // fc, width // dt
     any_space = pl.BlockSpec(memory_space=pl.ANY)
     dma = pltpu.SemaphoreType.DMA
@@ -926,10 +931,10 @@
     results = pl.pallas_call(
         hand_over,
         out_shape=[jax.ShapeDtypeStruct(*pair) for pair in shapes],
-        in_specs=[pl.BlockSpec(memory_space=pltpu.VMEM)] * 11,
-        out_specs=[any_space] * 11,
-        scratch_shapes=[dma((11,))],
-        compiler_params=pltpu.CompilerParams(vmem_limit_bytes=2**23),
+        in_specs=[pl.BlockSpec(memory_space=pltpu.HBM)] * 11,
+        out_specs=[pl.BlockSpec(memory_space=pltpu.HBM)] * 11,
+        scratch_shapes=[pltpu.VMEM(*pair) for pair in shapes] + [dma((11,)), dma((11,))],
+        compiler_params=pltpu.CompilerParams(vmem_limit_bytes=67043328),
     )(*results)
     output, grad_tokens, grg, gru, gde, geg, geu, gdr, gmg, gmu, gdm = results
     return (

time: 158 us -> 131 us (0.83)
  Pallas kernels: 146 us -> 130 us
  local copies, waits for them, and re-layouts: 10.1 us -> 0 us
    pallas_call x1, Pallas kernels: 144 us -> 127 us  [fused(): pl.pallas_call(kernel, out_shape=[jax.ShapeDtypeStruct(*pair) for pair in...]
    unnamed x22 -> x0, local copies, waits for them, and re-layouts: 10.1 us -> none
where the time goes in v2:
time: 131 us; the launch traced here: 130 us
  Pallas kernels  130 us (99%)
    pallas_call x1, Pallas kernels, fused(): pl.pallas_call(kernel, out_shape=[jax.ShapeDtypeStruct(*pair) for pair in...  127 us
    pallas_call x1, Pallas kernels, fused(): pl.pallas_call(hand_over, out_shape=[jax.ShapeDtypeStruct(*pair) for pair...  2.92 us

profile of v2, /device:TPU:0, one launch (start us, length us, event | category | flops | bytes accessed | tf_op | source)
XLA Modules:
  0.0 130.4 jit_solution(1351898919877791126)
XLA Ops:
  0.6 126.8 %shard_map.221 = (bf16[128,2048]{1,0:T(8,128)(2,1)}, bf16[128,2048]{1,0:T(8,128)(2,1)}, f32[32,2048]{1,0:T(8,128)}, f32[32,2048]{1,0:T(8,128)}, f32[32,2048]{1,0...) custom-call(bf16[128,2048]{1,0:T(8,128)(2,1)} %tok_hbm.1, ...), custom_call_target="tpu_custom_call" | custom-call | tf_op jit(solution)/shard_map/pallas_call | solution.py:856
  127.5 2.9 %shard_map.222 = (bf16[128,2048]{1,0:T(8,128)(2,1)}, bf16[128,2048]{1,0:T(8,128)(2,1)}, f32[32,2048]{1,0:T(8,128)}, f32[32,2048]{1,0:T(8,128)}, f32[32,2048]{1,0...) custom-call(bf16[128,2048]{1,0:T(8,128)(2,1)} %get-tuple-element.33., ...), custom_call_target="tpu_custom_call" | custom-call | tf_op jit(solution)/shard_map/pallas_call | solution.py:931
